TPU v7x, 512 devices: a 4x2x32 block of a 4x16x32 slice. The times are simulated.
512 devices in a mesh: group: 2 (over y), row: 64 (over z, core), col: 4 (over x).
Axes of the slice: x: 4, y: 2, z: 32, core: 2. Of those that a mesh axis runs over, the one named last changes fastest.
The devices are a block of a 4x16x32 slice.
Arguments:
- compressed_absorbed_queries: bfloat16 [256, 128, 512], P(('group', 'row')), parts along dimension 0, may hold values from -6 to 6
- query_rope: bfloat16 [256, 64, 128], P(('group', 'row')), parts along dimension 0, may hold values from -6 to 6
- compressed_stored_keys: bfloat16 [256, 1024, 512], P(('group', 'row'), 'col'), parts along dimension 0, may hold values from -32 to 32
- cache_rope: bfloat16 [256, 64, 1024], P(('group', 'row'), None, 'col'), parts along dimension 0, may hold values from -32 to 32
- seq_lengths: int32 [256], P(('group', 'row')), parts along dimension 0, may hold values from 2 to 1024, as said below
- ffn_rows: bfloat16 [1024, 7168], P(('group', 'row'), 'col'), parts along dimension 0, may hold values from -6 to 6
- norm_gain: bfloat16 [7168], P('col'), may hold values from 0.099609375 to 1.8984375
- w_gate: bfloat16 [7168, 18432], P('col', 'row'), may hold values from -0.0625 to 0.0625
- w_up: bfloat16 [7168, 18432], P('col', 'row'), may hold values from -0.0625 to 0.0625
- w_down: bfloat16 [18432, 7168], P('row', 'col'), may hold values from -0.046875 to 0.046875
Outputs:
- context: bfloat16 [256, 128, 512], P(('group', 'row'), 'col'), parts along dimension 0
- ffn_out: bfloat16 [1024, 7168], P(('group', 'row'), 'col'), parts along dimension 0
There are 2 independent parts, one for each index of `group`. A program takes and returns all parts, laid end to end along the dimension named above; an argument that names none is the same for every part. Nothing has to cross between parts.
Inputs may be any that keep to these rules, and one draw needn't show every extreme that they name: `seq_lengths`: each sequence has 2 to 1024 filled slots, the first ones of its cache, and some sequence has exactly 1024.
All inputs are finite; a program needn't handle non-finite values.
Results may differ from a plain program's by a relative error of at most 0.017.
Values may be sent and summed in bfloat16 or wider, within the bound.
No kernel may reach another device: no remote copies, remote signals or barrier semaphores. Data moves between devices by JAX's collectives and lax.ppermute only.
A program may use at most 64 MiB of HBM per device.

v0:
```python
import jax
import jax.numpy as jnp
from jax import lax
from jax.experimental.layout import Layout, with_layout_constraint
from jax.sharding import Mesh
from jax.sharding import PartitionSpec as P


NOPE = 128
FAR, NEAR, CORE, COL = "row_far", "row_near", "row_core", "col"
CHIP = (FAR, NEAR)
ROW = (FAR, NEAR, CORE)
GROUP_ROW = ("group", *ROW)
NEAR_CHIPS = 8

NEGATIVE_PADDING = -1e30


def row_major(x):
    return with_layout_constraint(x, Layout(major_to_minor=tuple(range(x.ndim))))


def on_lane(chip, lane):
    return 2 * chip + (lane + chip) % 2


def along_lane(x, hops_of_first, hops_of_second):
    chips = lax.axis_size(CHIP)
    pairs = [
        (on_lane(z, lane), on_lane((z + hops) % chips, lane))
        for lane, hops in enumerate((hops_of_first, hops_of_second))
        for z in range(chips)
    ]
    return lax.ppermute(x, ROW, pairs)


def gathered_on_lane(x):
    chips = lax.axis_size(CHIP)
    lanes = [[on_lane(z, lane) for z in range(chips)] for lane in (0, 1)]
    return lax.all_gather(x, ROW, axis_index_groups=lanes, axis=0, tiled=True)


def swapped(x):
    return lax.ppermute(x, CORE, [(0, 1), (1, 0)])


def exchanged(pieces):
    return lax.all_to_all(pieces, COL, split_axis=0, concat_axis=0, tiled=True)


def halves_of(x, count):
    pieces = []
    for _ in range(count - 1):
        coarse = lax.reduce_precision(x, 8, 7)
        pieces.append(coarse)
        x = x - coarse
    return pieces + [x]


def with_columns(x, columns):
    lane = lax.broadcasted_iota(jnp.int32, (*(1,) * (x.ndim - 1), 128), x.ndim - 1)
    extra = jnp.zeros((*x.shape[:-1], 128), jnp.float32)
    for k, column in enumerate(columns):
        extra = jnp.where(lane == k, column[..., None], extra)
    return jnp.concatenate([x.astype(jnp.bfloat16), extra.astype(jnp.bfloat16)], axis=-1)


def local_partials(
    compressed_absorbed_queries,
    query_rope,
    compressed_stored_keys,
    cache_rope,
    seq_lengths,
    first_pos,
):
    logits = jnp.einsum(
        "zxm,zum->zxu",
        compressed_absorbed_queries,
        compressed_stored_keys,
        preferred_element_type=jnp.float32,
    )
    logits = logits + jnp.einsum(
        "srh,srl->shl", query_rope, cache_rope, preferred_element_type=jnp.float32
    )
    logits = logits * (NOPE + query_rope.shape[1]) ** (-0.5)
    position = first_pos + jnp.arange(compressed_stored_keys.shape[1], dtype=jnp.int32)
    visible = position[None, None, :] < seq_lengths[:, None, None]
    logits = jnp.where(visible, logits, NEGATIVE_PADDING)
    top_score = jnp.max(logits, axis=2)
    weights = jnp.where(visible, jnp.exp(logits - top_score[:, :, None]), 0.0)
    denominator = jnp.sum(weights, axis=2)
    weighted = jnp.einsum(
        "jac,jcw->jaw",
        weights.astype(jnp.bfloat16),
        compressed_stored_keys,
        preferred_element_type=jnp.float32,
    )
    return top_score, denominator, weighted


def packed_attention(queries, query_rope, keys, cache_rope, seq_lengths, column):
    cols = lax.axis_size(COL)
    seqs, heads, _ = queries.shape
    top_score, denominator, weighted = local_partials(
        queries, query_rope, keys, cache_rope, seq_lengths, column * keys.shape[1]
    )
    packed = with_columns(weighted, halves_of(top_score, 3) + halves_of(denominator, 3))
    return jnp.moveaxis(packed.reshape(seqs, cols, heads // cols, -1), 1, 0)


def merged_attention(packed, latent, column):
    cols = lax.axis_size(COL)
    merged = []
    for k in range(cols):
        piece = lax.dynamic_index_in_dim(packed, (column + k) % cols, 0, keepdims=False)
        if k:
            piece = lax.ppermute(piece, COL, [(c, (c + k) % cols) for c in range(cols)])
        merged.append(piece.astype(jnp.float32))
    tops = [m[..., latent] + (m[..., latent + 1] + m[..., latent + 2]) for m in merged]
    totals = [m[..., latent + 3] + (m[..., latent + 4] + m[..., latent + 5]) for m in merged]
    top = tops[0]
    for other in tops[1:]:
        top = jnp.maximum(top, other)
    factors = [jnp.exp(t - top) for t in tops]
    total = sum(t * f for t, f in zip(totals, factors))
    context = sum(m[..., :latent] * f[..., None] for m, f in zip(merged, factors))
    return (context / total[..., None]).astype(jnp.bfloat16)


def summed_near(partial):
    near = lax.axis_index(NEAR)
    size = lax.axis_size(NEAR)

    def block(hops):
        return lax.dynamic_index_in_dim(partial, (near + hops) % size, 1, keepdims=False)

    half = size // 2
    arrived = [along_lane(block(half), half, -half)]
    for hops in range(half - 1, 0, -1):
        arrived += [along_lane(block(hops), hops, hops), along_lane(block(size - hops), -hops, -hops)]
    total = block(0).astype(jnp.float32)
    for other in arrived:
        total = total + other.astype(jnp.float32)
    return total.astype(jnp.bfloat16)


def feed_forward(ffn_rows, norm_gain, w_gate, w_up, w_down, queries):
    cols = lax.axis_size(COL)
    rows, width = ffn_rows.shape
    units = w_gate.shape[1]
    share = units // cols
    into = [w_gate.T, w_up.T]
    into += [swapped(w) for w in into]
    gathered = gathered_on_lane(ffn_rows)

    tokens = gathered.astype(jnp.float32)
    squares = jnp.sum(tokens * tokens, axis=1)
    scaled = (tokens * norm_gain.astype(jnp.float32)[None, :]).astype(jnp.bfloat16)
    packed = [
        lax.dot_general(w, scaled, (((1,), (1,)), ((), ())), preferred_element_type=jnp.float32)
        .astype(jnp.bfloat16)
        .reshape(cols, share, -1)
        for w in into
    ]
    norms = jnp.stack(halves_of(squares, 2)).astype(jnp.bfloat16)
    norms = jnp.pad(norms, ((0, 6), (0, 0)))
    packed.append(jnp.broadcast_to(norms, (cols, *norms.shape)))
    packed = row_major(jnp.concatenate(packed, axis=1))
    packed, w_down, queries = lax.optimization_barrier((packed, w_down, queries))
    out_of = [w_down, swapped(w_down)]
    total = exchanged(packed)
    total = jnp.sum(total.astype(jnp.float32), axis=0)
    mean_square = (total[4 * share] + total[4 * share + 1]) / (width * cols)
    scale = lax.rsqrt(mean_square + 1e-06)[None, :]
    total = (total[: 4 * share] * scale).reshape(2, 2, share, -1)
    hidden = (jax.nn.silu(total[:, 0]) * total[:, 1]).astype(jnp.bfloat16)

    hidden = exchanged(row_major(jnp.broadcast_to(hidden, (cols, *hidden.shape))))
    partial = sum(
        lax.dot_general(
            hidden[:, k].reshape(units, -1),
            w,
            (((0,), (0,)), ((), ())),
            preferred_element_type=jnp.float32,
        )
        for k, w in enumerate(out_of)
    )
    partial = partial.astype(jnp.bfloat16)
    partial = partial.reshape(lax.axis_size(FAR), lax.axis_size(NEAR), rows, width)
    return partial, queries


def on_device(
    compressed_absorbed_queries,
    query_rope,
    compressed_stored_keys,
    cache_rope,
    seq_lengths,
    ffn_rows,
    norm_gain,
    w_gate,
    w_up,
    w_down,
):
    column = lax.axis_index(COL)
    partial, queries = feed_forward(
        ffn_rows, norm_gain, w_gate, w_up, w_down, compressed_absorbed_queries
    )
    packed = packed_attention(
        queries, query_rope, compressed_stored_keys, cache_rope, seq_lengths, column
    )
    near = summed_near(partial)
    pieces = lax.all_to_all(row_major(near), FAR, 0, 0, tiled=True)
    reduced = jnp.sum(pieces.astype(jnp.float32), axis=0)
    context = merged_attention(packed, queries.shape[-1], column)
    ffn_out = (ffn_rows.astype(jnp.float32) + reduced).astype(jnp.bfloat16)
    return (context, ffn_out)


def solution(mesh):
    chips = mesh.shape["row"] // 2
    finer = Mesh(
        mesh.devices.reshape(
            mesh.shape["group"], chips // NEAR_CHIPS, NEAR_CHIPS, 2, mesh.shape["col"]
        ),
        ("group", *ROW, COL),
    )
    return jax.shard_map(
        on_device,
        mesh=finer,
        in_specs=(
            P(GROUP_ROW, None, None),
            P(GROUP_ROW, None, None),
            P(GROUP_ROW, COL, None),
            P(GROUP_ROW, None, COL),
            P(GROUP_ROW),
            P(GROUP_ROW, COL),
            P(COL),
            P(COL, ROW),
            P(COL, ROW),
            P(ROW, COL),
        ),
        out_specs=(P(GROUP_ROW, COL, None), P(GROUP_ROW, COL)),
        check_vma=False,
    )
```

profile of v0, /device:TPU:170, one launch (start us, length us, event | category | flops | bytes accessed | tf_op | source)
XLA Modules:
  0.0 204.7 jit_solution(13622626398083213749)
XLA Ops:
  0.7 2.1 %collective-permute-start = (bf16[288,1792]{1,0:T(8,128)(2,1)}, bf16[288,1792]{1,0:T(8,128)(2,1)}, u32[]{:S(2)}, u32[]{:S(2)}) collective-permute-start(bf16[288,1792]{1,0:T(8,128)(2,1)} %bitcast.88), channel_id=1, source_target_pairs={{0,4},{4,0},{1,5},{5,1},{2,6},{6,2},{3,7},{7,3},{8,12},{12,8},{9,1... | collective-permute-start | bytes 3096584 | tf_op jit(solution)/shard_map/ppermute | solution.py:44
  2.7 2.4 %collective-permute-start.1 = (bf16[288,1792]{1,0:T(8,128)(2,1)}, bf16[288,1792]{1,0:T(8,128)(2,1)}, u32[]{:S(2)}, u32[]{:S(2)}) collective-permute-start(bf16[288,1792]{1,0:T(8,128)(2,1)} %bitcast.89), channel_id=1, source_target_pairs={{0,4},{4,0},{1,5},{5,1},{2,6},{6,2},{3,7},{7,3},{8,12},{12,8},{9,1... | collective-permute-start | bytes 3096584 | tf_op jit(solution)/shard_map/ppermute | solution.py:44
  5.4 89.0 %all_gather.3 = bf16[256,1792]{1,0:T(8,128)(2,1)S(1)} all-gather(bf16[8,1792]{1,0:T(8,128)(2,1)} %param.15), channel_id=1, replica_groups={{0,12,16,28,32,44,48,60,64,76,80,92,96,108,112,124,128,140,144,156,160,..., dimensions={0}, use_global_device_ids=true | all-gather | bytes 946176 | tf_op jit(solution)/shard_map/all_gather | solution.py:40
  103.5 5.0 %all-to-all-start = ((bf16[4,296,256]{2,1,0:T(8,128)(2,1)}), bf16[4,296,256]{2,1,0:T(8,128)(2,1)S(1)}, u32[]{:S(2)}, u32[]{:S(2)}) async-start(bf16[4,296,256]{2,1,0:T(8,128)(2,1)} %constant_dynamic-update-slice_fusion), calls=%async_computation | async-start | bytes 1212416 | tf_op jit(solution)/shard_map/all_to_all | solution.py:48
  108.5 1.9 collective-permute-start.5
  111.4 6.3 %all-to-all-done = bf16[4,296,256]{2,1,0:T(8,128)(2,1)S(1)} async-done(((bf16[4,296,256]{2,1,0:T(8,128)(2,1)}), bf16[4,296,256]{2,1,0:T(8,128)(2,1)S(1)}, u32[]{:S(2)}, u32[]{:S(2)}) %all-to-all-start) | async-done | bytes 606240 | tf_op jit(solution)/shard_map/all_to_all | solution.py:48
  118.6 4.9 %all-to-all-start.1 = ((bf16[4,2,72,256]{3,2,1,0:T(8,128)(2,1)}), bf16[4,2,72,256]{3,2,1,0:T(8,128)(2,1)S(1)}, u32[]{:S(2)}, u32[]{:S(2)}) async-start(bf16[4,2,72,256]{3,2,1,0:T(8,128)(2,1)} %broadcast_in_dim.126), calls=%async_computation.1 | async-start | bytes 589824 | tf_op jit(solution)/shard_map/all_to_all | solution.py:48
  123.5 5.4 %all-to-all-done.1 = bf16[4,2,72,256]{3,2,1,0:T(8,128)(2,1)S(1)} async-done(((bf16[4,2,72,256]{3,2,1,0:T(8,128)(2,1)}), bf16[4,2,72,256]{3,2,1,0:T(8,128)(2,1)S(1)}, u32[]{:S(2)}, u32[]{:S(2)}) %all-to-all-start.1) | async-done | bytes 294944 | tf_op jit(solution)/shard_map/all_to_all | solution.py:48
  129.6 1.9 fusion
  131.6 4.1 %collective-permute-start.10 = (bf16[4,8,1792]{2,1,0:T(8,128)(2,1)S(1)}, bf16[4,8,1792]{2,1,0:T(8,128)(2,1)S(1)}, u32[]{:S(2)}, u32[]{:S(2)}) collective-permute-start(bf16[4,8,1792]{2,1,0:T(8,128)(2,1)S(1)} %get-tuple-element.21), channel_id=1, source_target_pairs={{0,240},{12,252},{16,0},{28,12},{32,16},{44,28},{48,32},{60,44},{6... | collective-permute-start | bytes 344072 | tf_op jit(solution)/shard_map/ppermute | solution.py:34
  135.7 2.0 collective-permute-start.11
  137.9 3.6 %collective-permute-start.12 = (bf16[4,8,1792]{2,1,0:T(8,128)(2,1)S(1)}, bf16[4,8,1792]{2,1,0:T(8,128)(2,1)S(1)}, u32[]{:S(2)}, u32[]{:S(2)}) collective-permute-start(bf16[4,8,1792]{2,1,0:T(8,128)(2,1)S(1)} %get-tuple-element.19), channel_id=1, source_target_pairs={{0,252},{12,0},{16,12},{28,16},{32,28},{44,32},{48,44},{60,48},{64... | collective-permute-start | bytes 344072 | tf_op jit(solution)/shard_map/ppermute | solution.py:34
  141.6 3.8 %collective-permute-start.6 = (bf16[4,8,1792]{2,1,0:T(8,128)(2,1)S(1)}, bf16[4,8,1792]{2,1,0:T(8,128)(2,1)S(1)}, u32[]{:S(2)}, u32[]{:S(2)}) collective-permute-start(bf16[4,8,1792]{2,1,0:T(8,128)(2,1)S(1)} %get-tuple-element.18), channel_id=1, source_target_pairs={{0,32},{12,44},{16,48},{28,60},{32,64},{44,76},{48,80},{60,92},{64... | collective-permute-start | bytes 344072 | tf_op jit(solution)/shard_map/ppermute | solution.py:34
  145.4 4.8 %collective-permute-start.7 = (bf16[4,8,1792]{2,1,0:T(8,128)(2,1)S(1)}, bf16[4,8,1792]{2,1,0:T(8,128)(2,1)S(1)}, u32[]{:S(2)}, u32[]{:S(2)}) collective-permute-start(bf16[4,8,1792]{2,1,0:T(8,128)(2,1)S(1)} %get-tuple-element.24), channel_id=1, source_target_pairs={{0,28},{12,32},{16,44},{28,48},{32,60},{44,64},{48,76},{60,80},{64... | collective-permute-start | bytes 344072 | tf_op jit(solution)/shard_map/ppermute | solution.py:34
  150.2 3.9 %collective-permute-start.8 = (bf16[4,8,1792]{2,1,0:T(8,128)(2,1)S(1)}, bf16[4,8,1792]{2,1,0:T(8,128)(2,1)S(1)}, u32[]{:S(2)}, u32[]{:S(2)}) collective-permute-start(bf16[4,8,1792]{2,1,0:T(8,128)(2,1)S(1)} %get-tuple-element.23), channel_id=1, source_target_pairs={{0,236},{12,240},{16,252},{28,0},{32,12},{44,16},{48,28},{60,32},{... | collective-permute-start | bytes 344072 | tf_op jit(solution)/shard_map/ppermute | solution.py:34
  154.1 2.2 %collective-permute-start.9 = (bf16[4,8,1792]{2,1,0:T(8,128)(2,1)S(1)}, bf16[4,8,1792]{2,1,0:T(8,128)(2,1)S(1)}, u32[]{:S(2)}, u32[]{:S(2)}) collective-permute-start(bf16[4,8,1792]{2,1,0:T(8,128)(2,1)S(1)} %get-tuple-element.22), channel_id=1, source_target_pairs={{0,16},{12,28},{16,32},{28,44},{32,48},{44,60},{48,64},{60,76},{64... | collective-permute-start | bytes 344072 | tf_op jit(solution)/shard_map/ppermute | solution.py:34
  156.3 3.9 %collective-permute-done.7 = bf16[4,8,1792]{2,1,0:T(8,128)(2,1)S(1)} collective-permute-done((bf16[4,8,1792]{2,1,0:T(8,128)(2,1)S(1)}, bf16[4,8,1792]{2,1,0:T(8,128)(2,1)S(1)}, u32[]{:S(2)}, u32[]{:S(2)}) %collective-permute-start.7) | collective-permute-done | bytes 114720 | tf_op jit(solution)/shard_map/ppermute | solution.py:34
  161.2 5.5 %collective-permute-done.9 = bf16[4,8,1792]{2,1,0:T(8,128)(2,1)S(1)} collective-permute-done((bf16[4,8,1792]{2,1,0:T(8,128)(2,1)S(1)}, bf16[4,8,1792]{2,1,0:T(8,128)(2,1)S(1)}, u32[]{:S(2)}, u32[]{:S(2)}) %collective-permute-start.9) | collective-permute-done | bytes 114720 | tf_op jit(solution)/shard_map/ppermute | solution.py:34
  167.4 6.4 %all-to-all-start.2 = ((bf16[4,8,1792]{2,1,0:T(8,128)(2,1)}), bf16[4,8,1792]{2,1,0:T(8,128)(2,1)S(1)}, u32[]{:S(2)}, u32[]{:S(2)}) async-start(bf16[4,8,1792]{2,1,0:T(8,128)(2,1)} %fusion.15), calls=%async_computation.2 | async-start | bytes 229376 | tf_op jit(solution)/shard_map/all_to_all | solution.py:213
  173.8 2.0 collective-permute-start.2
  175.8 5.5 %collective-permute-start.3 = (bf16[2,32,640]{2,1,0:T(8,128)(2,1)S(1)}, bf16[2,32,640]{2,1,0:T(8,128)(2,1)S(1)}, u32[]{:S(2)}, u32[]{:S(2)}) collective-permute-start(bf16[2,32,640]{2,1,0:T(8,128)(2,1)S(1)} %get-tuple-element.27), channel_id=1, source_target_pairs={{0,2},{1,3},{2,0},{3,1},{4,6},{5,7},{6,4},{7,5},{8,10},{9,11},{10,... | collective-permute-start | bytes 245768 | tf_op jit(solution)/shard_map/ppermute | solution.py:117
  181.3 2.4 %collective-permute-start.4 = (bf16[2,32,640]{2,1,0:T(8,128)(2,1)S(1)}, bf16[2,32,640]{2,1,0:T(8,128)(2,1)S(1)}, u32[]{:S(2)}, u32[]{:S(2)}) collective-permute-start(bf16[2,32,640]{2,1,0:T(8,128)(2,1)S(1)} %get-tuple-element.26), channel_id=1, source_target_pairs={{0,3},{1,0},{2,1},{3,2},{4,7},{5,4},{6,5},{7,6},{8,11},{9,8},{10,9... | collective-permute-start | bytes 245768 | tf_op jit(solution)/shard_map/ppermute | solution.py:117
  184.2 3.5 %collective-permute-done.4 = bf16[2,32,640]{2,1,0:T(8,128)(2,1)S(1)} collective-permute-done((bf16[2,32,640]{2,1,0:T(8,128)(2,1)S(1)}, bf16[2,32,640]{2,1,0:T(8,128)(2,1)S(1)}, u32[]{:S(2)}, u32[]{:S(2)}) %collective-permute-start.4) | collective-permute-done | bytes 81952 | tf_op jit(solution)/shard_map/ppermute | solution.py:117
  188.8 15.2 %all-to-all-done.2 = bf16[4,8,1792]{2,1,0:T(8,128)(2,1)S(1)} async-done(((bf16[4,8,1792]{2,1,0:T(8,128)(2,1)}), bf16[4,8,1792]{2,1,0:T(8,128)(2,1)S(1)}, u32[]{:S(2)}, u32[]{:S(2)}) %all-to-all-start.2) | async-done | bytes 114720 | tf_op jit(solution)/shard_map/all_to_all | solution.py:213
  (71 shorter events, 16.0 us)
Async XLA Ops:
  0.6 109.8 %copy-start = (bf16[2,256,512]{2,1,0:T(8,128)(2,1)S(1)}, bf16[2,256,512]{2,1,0:T(8,128)(2,1)}, u32[]{:S(2)}) copy-start(bf16[2,256,512]{2,1,0:T(8,128)(2,1)} %param.12) | copy-start | bytes 1572868
  0.6 94.6 %copy-start.7 = (bf16[1792,288]{0,1:T(8,128)(2,1)S(1)}, bf16[1792,288]{0,1:T(8,128)(2,1)}, u32[]{:S(2)}) copy-start(bf16[1792,288]{0,1:T(8,128)(2,1)} %param.17) | copy-start | bytes 3096580
  0.7 97.4 %collective-permute-start = (bf16[288,1792]{1,0:T(8,128)(2,1)}, bf16[288,1792]{1,0:T(8,128)(2,1)}, u32[]{:S(2)}, u32[]{:S(2)}) collective-permute-start(bf16[288,1792]{1,0:T(8,128)(2,1)} %bitcast.88), channel_id=1, source_target_pairs={{0,4},{4,0},{1,5},{5,1},{2,6},{6,2},{3,7},{7,3},{8,12},{12,8},{9,1... | collective-permute-start | bytes 3096584 | tf_op jit(solution)/shard_map/ppermute | solution.py:44
  2.7 97.7 %collective-permute-start.1 = (bf16[288,1792]{1,0:T(8,128)(2,1)}, bf16[288,1792]{1,0:T(8,128)(2,1)}, u32[]{:S(2)}, u32[]{:S(2)}) collective-permute-start(bf16[288,1792]{1,0:T(8,128)(2,1)} %bitcast.89), channel_id=1, source_target_pairs={{0,4},{4,0},{1,5},{5,1},{2,6},{6,2},{3,7},{7,3},{8,12},{12,8},{9,1... | collective-permute-start | bytes 3096584 | tf_op jit(solution)/shard_map/ppermute | solution.py:44
  95.8 2.0 copy-start.6
  95.8 2.0 copy-start.4
  95.8 2.0 copy-start.5
  100.4 8.1 %copy-start.1 = (bf16[288,1792]{1,0:T(8,128)(2,1)S(1)}, bf16[288,1792]{1,0:T(8,128)(2,1)}, u32[]{:S(2)}) copy-start(bf16[288,1792]{1,0:T(8,128)(2,1)} %param.19) | copy-start | bytes 3096580
  100.4 10.0 %copy-start.2 = (bf16[2,128,512]{2,1,0:T(8,128)(2,1)S(1)}, bf16[2,128,512]{2,1,0:T(8,128)(2,1)}, u32[]{:S(2)}) copy-start(bf16[2,128,512]{2,1,0:T(8,128)(2,1)} %param.10) | copy-start | bytes 786436
  103.5 14.1 %all-to-all-start = ((bf16[4,296,256]{2,1,0:T(8,128)(2,1)}), bf16[4,296,256]{2,1,0:T(8,128)(2,1)S(1)}, u32[]{:S(2)}, u32[]{:S(2)}) async-start(bf16[4,296,256]{2,1,0:T(8,128)(2,1)} %constant_dynamic-update-slice_fusion), calls=%async_computation | async-start | bytes 1212416 | tf_op jit(solution)/shard_map/all_to_all | solution.py:48
  108.5 21.1 %collective-permute-start.5 = (bf16[288,1792]{1,0:T(8,128)(2,1)S(1)}, bf16[288,1792]{1,0:T(8,128)(2,1)}, u32[]{:S(2)}, u32[]{:S(2)}) collective-permute-start(bf16[288,1792]{1,0:T(8,128)(2,1)S(1)} %copy-done.1), channel_id=1, source_target_pairs={{0,4},{4,0},{1,5},{5,1},{2,6},{6,2},{3,7},{7,3},{8,12},{12,8},{9,1... | collective-permute-start | bytes 3096584 | tf_op jit(solution)/shard_map/ppermute | solution.py:44
  118.6 10.3 %all-to-all-start.1 = ((bf16[4,2,72,256]{3,2,1,0:T(8,128)(2,1)}), bf16[4,2,72,256]{3,2,1,0:T(8,128)(2,1)S(1)}, u32[]{:S(2)}, u32[]{:S(2)}) async-start(bf16[4,2,72,256]{3,2,1,0:T(8,128)(2,1)} %broadcast_in_dim.126), calls=%async_computation.1 | async-start | bytes 589824 | tf_op jit(solution)/shard_map/all_to_all | solution.py:48
  131.6 18.6 %collective-permute-start.10 = (bf16[4,8,1792]{2,1,0:T(8,128)(2,1)S(1)}, bf16[4,8,1792]{2,1,0:T(8,128)(2,1)S(1)}, u32[]{:S(2)}, u32[]{:S(2)}) collective-permute-start(bf16[4,8,1792]{2,1,0:T(8,128)(2,1)S(1)} %get-tuple-element.21), channel_id=1, source_target_pairs={{0,240},{12,252},{16,0},{28,12},{32,16},{44,28},{48,32},{60,44},{6... | collective-permute-start | bytes 344072 | tf_op jit(solution)/shard_map/ppermute | solution.py:34
  135.7 18.4 %collective-permute-start.11 = (bf16[4,8,1792]{2,1,0:T(8,128)(2,1)S(1)}, bf16[4,8,1792]{2,1,0:T(8,128)(2,1)S(1)}, u32[]{:S(2)}, u32[]{:S(2)}) collective-permute-start(bf16[4,8,1792]{2,1,0:T(8,128)(2,1)S(1)} %get-tuple-element.20), channel_id=1, source_target_pairs={{0,12},{12,16},{16,28},{28,32},{32,44},{44,48},{48,60},{60,64},{64... | collective-permute-start | bytes 344072 | tf_op jit(solution)/shard_map/ppermute | solution.py:34
  137.9 18.4 %collective-permute-start.12 = (bf16[4,8,1792]{2,1,0:T(8,128)(2,1)S(1)}, bf16[4,8,1792]{2,1,0:T(8,128)(2,1)S(1)}, u32[]{:S(2)}, u32[]{:S(2)}) collective-permute-start(bf16[4,8,1792]{2,1,0:T(8,128)(2,1)S(1)} %get-tuple-element.19), channel_id=1, source_target_pairs={{0,252},{12,0},{16,12},{28,16},{32,28},{44,32},{48,44},{60,48},{64... | collective-permute-start | bytes 344072 | tf_op jit(solution)/shard_map/ppermute | solution.py:34
  141.6 14.8 %collective-permute-start.6 = (bf16[4,8,1792]{2,1,0:T(8,128)(2,1)S(1)}, bf16[4,8,1792]{2,1,0:T(8,128)(2,1)S(1)}, u32[]{:S(2)}, u32[]{:S(2)}) collective-permute-start(bf16[4,8,1792]{2,1,0:T(8,128)(2,1)S(1)} %get-tuple-element.18), channel_id=1, source_target_pairs={{0,32},{12,44},{16,48},{28,60},{32,64},{44,76},{48,80},{60,92},{64... | collective-permute-start | bytes 344072 | tf_op jit(solution)/shard_map/ppermute | solution.py:34
  145.4 14.8 %collective-permute-start.7 = (bf16[4,8,1792]{2,1,0:T(8,128)(2,1)S(1)}, bf16[4,8,1792]{2,1,0:T(8,128)(2,1)S(1)}, u32[]{:S(2)}, u32[]{:S(2)}) collective-permute-start(bf16[4,8,1792]{2,1,0:T(8,128)(2,1)S(1)} %get-tuple-element.24), channel_id=1, source_target_pairs={{0,28},{12,32},{16,44},{28,48},{32,60},{44,64},{48,76},{60,80},{64... | collective-permute-start | bytes 344072 | tf_op jit(solution)/shard_map/ppermute | solution.py:34
  150.2 11.0 %collective-permute-start.8 = (bf16[4,8,1792]{2,1,0:T(8,128)(2,1)S(1)}, bf16[4,8,1792]{2,1,0:T(8,128)(2,1)S(1)}, u32[]{:S(2)}, u32[]{:S(2)}) collective-permute-start(bf16[4,8,1792]{2,1,0:T(8,128)(2,1)S(1)} %get-tuple-element.23), channel_id=1, source_target_pairs={{0,236},{12,240},{16,252},{28,0},{32,12},{44,16},{48,28},{60,32},{... | collective-permute-start | bytes 344072 | tf_op jit(solution)/shard_map/ppermute | solution.py:34
  154.1 12.6 %collective-permute-start.9 = (bf16[4,8,1792]{2,1,0:T(8,128)(2,1)S(1)}, bf16[4,8,1792]{2,1,0:T(8,128)(2,1)S(1)}, u32[]{:S(2)}, u32[]{:S(2)}) collective-permute-start(bf16[4,8,1792]{2,1,0:T(8,128)(2,1)S(1)} %get-tuple-element.22), channel_id=1, source_target_pairs={{0,16},{12,28},{16,32},{28,44},{32,48},{44,60},{48,64},{60,76},{64... | collective-permute-start | bytes 344072 | tf_op jit(solution)/shard_map/ppermute | solution.py:34
  167.4 36.7 %copy-start.3 = (bf16[8,1792]{1,0:T(8,128)(2,1)S(1)}, bf16[8,1792]{1,0:T(8,128)(2,1)}, u32[]{:S(2)}) copy-start(bf16[8,1792]{1,0:T(8,128)(2,1)} %param.15) | copy-start | bytes 86020
  167.4 36.7 %all-to-all-start.2 = ((bf16[4,8,1792]{2,1,0:T(8,128)(2,1)}), bf16[4,8,1792]{2,1,0:T(8,128)(2,1)S(1)}, u32[]{:S(2)}, u32[]{:S(2)}) async-start(bf16[4,8,1792]{2,1,0:T(8,128)(2,1)} %fusion.15), calls=%async_computation.2 | async-start | bytes 229376 | tf_op jit(solution)/shard_map/all_to_all | solution.py:213
  173.8 9.8 %collective-permute-start.2 = (bf16[2,32,640]{2,1,0:T(8,128)(2,1)S(1)}, bf16[2,32,640]{2,1,0:T(8,128)(2,1)S(1)}, u32[]{:S(2)}, u32[]{:S(2)}) collective-permute-start(bf16[2,32,640]{2,1,0:T(8,128)(2,1)S(1)} %get-tuple-element.28), channel_id=1, source_target_pairs={{0,1},{1,2},{2,3},{3,0},{4,5},{5,6},{6,7},{7,4},{8,9},{9,10},{10,1... | collective-permute-start | bytes 245768 | tf_op jit(solution)/shard_map/ppermute | solution.py:117
  175.8 8.3 %collective-permute-start.3 = (bf16[2,32,640]{2,1,0:T(8,128)(2,1)S(1)}, bf16[2,32,640]{2,1,0:T(8,128)(2,1)S(1)}, u32[]{:S(2)}, u32[]{:S(2)}) collective-permute-start(bf16[2,32,640]{2,1,0:T(8,128)(2,1)S(1)} %get-tuple-element.27), channel_id=1, source_target_pairs={{0,2},{1,3},{2,0},{3,1},{4,6},{5,7},{6,4},{7,5},{8,10},{9,11},{10,... | collective-permute-start | bytes 245768 | tf_op jit(solution)/shard_map/ppermute | solution.py:117
  181.3 6.4 %collective-permute-start.4 = (bf16[2,32,640]{2,1,0:T(8,128)(2,1)S(1)}, bf16[2,32,640]{2,1,0:T(8,128)(2,1)S(1)}, u32[]{:S(2)}, u32[]{:S(2)}) collective-permute-start(bf16[2,32,640]{2,1,0:T(8,128)(2,1)S(1)} %get-tuple-element.26), channel_id=1, source_target_pairs={{0,3},{1,0},{2,1},{3,2},{4,7},{5,4},{6,5},{7,6},{8,11},{9,8},{10,9... | collective-permute-start | bytes 245768 | tf_op jit(solution)/shard_map/ppermute | solution.py:117
  (1 other events, 1.5 us)
where the time goes:
time: 206 us; the launch traced here: 205 us
  blocking collectives  89 us (43%)
  starting transfers between devices  56.9 us (28%)
  waiting for transfers between devices  41.2 us (20%)
  matrix products  7.88 us (4%)
  other arithmetic  4.38 us (2%)
  local copies, waits for them, and re-layouts  4.2 us (2%)
    all_gather x1, blocking collectives, gathered_on_lane(): return lax.all_gather(x, ROW, axis_index_groups=lanes, axis=0, tiled=True)  89 us
    ppermute x7, starting transfers between devices, along_lane(): return lax.ppermute(x, ROW, pairs)  24.4 us
    all_to_all x1, waiting for transfers between devices, on_device(): pieces = lax.all_to_all(row_major(near), FAR, 0, 0, tiled=True)  15.2 us
    all_to_all x2, waiting for transfers between devices, exchanged(): return lax.all_to_all(pieces, COL, split_axis=0, concat_axis=0, tiled=True)  11.7 us
    ppermute x7, waiting for transfers between devices, along_lane(): return lax.ppermute(x, ROW, pairs)  10.3 us
    all_to_all x2, starting transfers between devices, exchanged(): return lax.all_to_all(pieces, COL, split_axis=0, concat_axis=0, tiled=True)  9.87 us
    ppermute x3, starting transfers between devices, merged_attention(): piece = lax.ppermute(piece, COL, [(c, (c + k) % cols) for c in range(cols)])  9.81 us
    ppermute x3, starting transfers between devices, swapped(): return lax.ppermute(x, CORE, [(0, 1), (1, 0)])  6.46 us
  transfers between devices with their start and end apart: 16, of which 8 were waited for; matrix products, arithmetic and copies ran while one was open for 5% of the time, Pallas kernels for 0%

commit v1 on v0

--- a/solution.py
+++ b/solution.py
@@ -1,6 +1,8 @@
 import jax
 import jax.numpy as jnp
 from jax import lax
+from jax.experimental import pallas as pl
+from jax.experimental.pallas import tpu as pltpu
 from jax.experimental.layout import Layout, with_layout_constraint
 from jax.sharding import Mesh
 from jax.sharding import PartitionSpec as P
@@ -128,20 +130,85 @@
 
 
 def summed_near(partial):
+    far, size = partial.shape[:2]
     near = lax.axis_index(NEAR)
-    size = lax.axis_size(NEAR)
-
-    def block(hops):
-        return lax.dynamic_index_in_dim(partial, (near + hops) % size, 1, keepdims=False)
-
-    half = size // 2
-    arrived = [along_lane(block(half), half, -half)]
+    window = size // 2
+    place, side = near % window, near // window
+    partial = partial.reshape(2 * far, window, *partial.shape[2:])
+
+    def block(blocks, k):
+        return lax.dynamic_index_in_dim(blocks, k, 1, keepdims=False)
+
+    half = window // 2
+    arrived = [along_lane(block(partial, (place + half) % window), half, -half)]
     for hops in range(half - 1, 0, -1):
-        arrived += [along_lane(block(hops), hops, hops), along_lane(block(size - hops), -hops, -hops)]
-    total = block(0).astype(jnp.float32)
+        arrived += [
+            along_lane(block(partial, (place + hops) % window), hops, hops),
+            along_lane(block(partial, (place + window - hops) % window), -hops, -hops),
+        ]
+    total = block(partial, place).astype(jnp.float32)
     for other in arrived:
         total = total + other.astype(jnp.float32)
+    total = total.astype(jnp.bfloat16).reshape(far, 2, *partial.shape[2:])
+    other = along_lane(block(total, 1 - side), window, -window)
+    total = block(total, side).astype(jnp.float32) + other.astype(jnp.float32)
     return total.astype(jnp.bfloat16)
+
+
+def project_kernel(x_ref, gain_ref, *refs):
+    *w_refs, out_ref, w_vmem, arrived = refs
+    copies = [
+        pltpu.make_async_copy(w_ref, w_vmem.at[k], arrived.at[k]) for k, w_ref in enumerate(w_refs)
+    ]
+    for copy in copies:
+        copy.start()
+    cols, _, _ = out_ref.shape
+    share = w_vmem.shape[1] // cols
+    x = x_ref[...].astype(jnp.float32)
+    scaled = (x * gain_ref[...].astype(jnp.float32)).astype(jnp.bfloat16)
+    squares = lax.dot_general(
+        jnp.ones((8, x.shape[1]), jnp.float32),
+        x * x,
+        (((1,), (1,)), ((), ())),
+        precision=lax.Precision.HIGHEST,
+        preferred_element_type=jnp.float32,
+    )
+    coarse = squares.astype(jnp.bfloat16).astype(jnp.float32)
+    row = lax.broadcasted_iota(jnp.int32, squares.shape, 0)
+    norms = jnp.where(row == 0, coarse, squares - coarse).astype(jnp.bfloat16)
+    for c in range(cols):
+        out_ref[c, len(copies) * share :, :] = norms
+    for k, copy in enumerate(copies):
+        copy.wait()
+        product = lax.dot_general(
+            w_vmem[k], scaled, (((1,), (1,)), ((), ())), preferred_element_type=jnp.float32
+        ).astype(jnp.bfloat16)
+        for c in range(cols):
+            out_ref[c, k * share : (k + 1) * share, :] = product[c * share : (c + 1) * share, :]
+
+
+def projected(gathered, gain, weights, cols):
+    tokens, width = gathered.shape
+    units = weights[0].shape[0]
+    rows = len(weights) * units // cols + 8
+    whole = pl.BlockSpec(memory_space=pltpu.VMEM)
+    return pl.pallas_call(
+        project_kernel,
+        out_shape=jax.ShapeDtypeStruct((cols, rows, tokens), jnp.bfloat16),
+        in_specs=[whole, whole] + [pl.BlockSpec(memory_space=pltpu.HBM)] * len(weights),
+        out_specs=whole,
+        scratch_shapes=[
+            pltpu.VMEM((len(weights), units, width), jnp.bfloat16),
+            pltpu.SemaphoreType.DMA((len(weights),)),
+        ],
+        compiler_params=pltpu.CompilerParams(vmem_limit_bytes=24 << 20),
+        cost_estimate=pl.CostEstimate(
+            flops=2 * len(weights) * units * width * tokens,
+            bytes_accessed=2 * len(weights) * units * width,
+            transcendentals=0,
+        ),
+        name="projected",
+    )(gathered, gain[None, :], *weights)
 
 
 def feed_forward(ffn_rows, norm_gain, w_gate, w_up, w_down, queries):
@@ -153,20 +220,8 @@
     into += [swapped(w) for w in into]
     gathered = gathered_on_lane(ffn_rows)
 
-    tokens = gathered.astype(jnp.float32)
-    squares = jnp.sum(tokens * tokens, axis=1)
-    scaled = (tokens * norm_gain.astype(jnp.float32)[None, :]).astype(jnp.bfloat16)
-    packed = [
-        lax.dot_general(w, scaled, (((1,), (1,)), ((), ())), preferred_element_type=jnp.float32)
-        .astype(jnp.bfloat16)
-        .reshape(cols, share, -1)
-        for w in into
-    ]
-    norms = jnp.stack(halves_of(squares, 2)).astype(jnp.bfloat16)
-    norms = jnp.pad(norms, ((0, 6), (0, 0)))
-    packed.append(jnp.broadcast_to(norms, (cols, *norms.shape)))
-    packed = row_major(jnp.concatenate(packed, axis=1))
-    packed, w_down, queries = lax.optimization_barrier((packed, w_down, queries))
+    packed = projected(gathered, norm_gain, into, cols)
+    packed, w_down, *queries = lax.optimization_barrier((packed, w_down, *queries))
     out_of = [w_down, swapped(w_down)]
     total = exchanged(packed)
     total = jnp.sum(total.astype(jnp.float32), axis=0)
@@ -204,15 +259,20 @@
 ):
     column = lax.axis_index(COL)
     partial, queries = feed_forward(
-        ffn_rows, norm_gain, w_gate, w_up, w_down, compressed_absorbed_queries
+        ffn_rows,
+        norm_gain,
+        w_gate,
+        w_up,
+        w_down,
+        (compressed_absorbed_queries, query_rope),
     )
     packed = packed_attention(
-        queries, query_rope, compressed_stored_keys, cache_rope, seq_lengths, column
+        *queries, compressed_stored_keys, cache_rope, seq_lengths, column
     )
     near = summed_near(partial)
     pieces = lax.all_to_all(row_major(near), FAR, 0, 0, tiled=True)
     reduced = jnp.sum(pieces.astype(jnp.float32), axis=0)
-    context = merged_attention(packed, queries.shape[-1], column)
+    context = merged_attention(packed, compressed_stored_keys.shape[-1], column)
     ffn_out = (ffn_rows.astype(jnp.float32) + reduced).astype(jnp.bfloat16)
     return (context, ffn_out)
 

time: 206 us -> 200 us (0.971)
  the two profiles are of different devices: /device:TPU:170 before, /device:TPU:40 now
where the time goes in v1:
time: 200 us
  blocking collectives  92.8 us (46%)
  waiting for transfers between devices  49.2 us (25%)
  starting transfers between devices  36.5 us (18%)
  Pallas kernels  7.47 us (4%)
  other arithmetic  6.39 us (3%)
  local copies, waits for them, and re-layouts  3.31 us (2%)
  matrix products  2.9 us (1%)
    all_gather x1, blocking collectives, gathered_on_lane(): return lax.all_gather(x, ROW, axis_index_groups=lanes, axis=0, tiled=True)  92.8 us
    ppermute x4, waiting for transfers between devices, along_lane(): return lax.ppermute(x, ROW, pairs)  20.4 us
    all_to_all x2, waiting for transfers between devices, exchanged(): return lax.all_to_all(pieces, COL, split_axis=0, concat_axis=0, tiled=True)  13.8 us
    ppermute x4, starting transfers between devices, along_lane(): return lax.ppermute(x, ROW, pairs)  9.76 us
    all_to_all x1, waiting for transfers between devices, on_device(): pieces = lax.all_to_all(row_major(near), FAR, 0, 0, tiled=True)  9.47 us
    ppermute x3, starting transfers between devices, merged_attention(): piece = lax.ppermute(piece, COL, [(c, (c + k) % cols) for c in range(cols)])  8.48 us
    all_to_all x2, starting transfers between devices, exchanged(): return lax.all_to_all(pieces, COL, split_axis=0, concat_axis=0, tiled=True)  8.13 us
    pallas_call x1, Pallas kernels, projected(): pl.pallas_call(project_kernel, out_shape=jax.ShapeDtypeStruct((cols, rows...  7.47 us
  transfers between devices with their start and end apart: 13, of which 8 were waited for; matrix products, arithmetic and copies ran while one was open for 4% of the time, Pallas kernels for 0%

profile of v1, /device:TPU:40, one launch (start us, length us, event | category | flops | bytes accessed | tf_op | source)
XLA Modules:
  0.0 199.6 jit_solution(15924845333366800037)
XLA Ops:
  0.7 2.1 %collective-permute-start = (bf16[288,1792]{1,0:T(8,128)(2,1)}, bf16[288,1792]{1,0:T(8,128)(2,1)S(1)}, u32[]{:S(2)}, u32[]{:S(2)}) collective-permute-start(bf16[288,1792]{1,0:T(8,128)(2,1)} %bitcast.59), channel_id=1, source_target_pairs={{0,4},{4,0},{1,5},{5,1},{2,6},{6,2},{3,7},{7,3},{8,12},{12,8},{9,1... | collective-permute-start | bytes 3096584 | tf_op jit(solution)/shard_map/ppermute | solution.py:46
  2.7 2.4 %collective-permute-start.1 = (bf16[288,1792]{1,0:T(8,128)(2,1)}, bf16[288,1792]{1,0:T(8,128)(2,1)}, u32[]{:S(2)}, u32[]{:S(2)}) collective-permute-start(bf16[288,1792]{1,0:T(8,128)(2,1)} %bitcast.61), channel_id=1, source_target_pairs={{0,4},{4,0},{1,5},{5,1},{2,6},{6,2},{3,7},{7,3},{8,12},{12,8},{9,1... | collective-permute-start | bytes 3096584 | tf_op jit(solution)/shard_map/ppermute | solution.py:46
  7.6 1.3 broadcast_compare_fusion
  8.9 92.8 %all_gather.3.x_ref = bf16[256,1792]{1,0:T(8,128)(2,1)S(1)} all-gather(bf16[8,1792]{1,0:T(8,128)(2,1)} %param.15), channel_id=1, replica_groups={{0,12,16,28,32,44,48,60,64,76,80,92,96,108,112,124,128,140,144,156,160,..., dimensions={0}, use_global_device_ids=true | all-gather | bytes 946176 | tf_op jit(solution)/shard_map/all_gather | solution.py:42
  102.9 7.5 %projected.1 = bf16[4,296,256]{2,1,0:T(8,128)(2,1)} custom-call(bf16[256,1792]{1,0:T(8,128)(2,1)S(1)} %all_gather.3.x_ref, bf16[1,1792]{1,0:T(2,128)(2,1)S(1)} %broadcast_in_dim.109.gain_ref, bf16[288,1792]{1,0:T(8,128)(2,1)S(1)} %bitcast.60, bf16[288,1792]{1,0:T(8,128)(2,1)S(1)} %bitcast.62, bf16[288,1792]{1,0:T(8,128)(2,1)S(1)} %collective-permute-done.refs_2_, ...), custom_call_target="tpu_custom_call" | custom-call | flops 1056964608 | bytes 4128768 | tf_op jit(solution)/shard_map/projected/pallas_call | solution.py:195
  110.4 4.6 %all-to-all-start = ((bf16[4,296,256]{2,1,0:T(8,128)(2,1)}), bf16[4,296,256]{2,1,0:T(8,128)(2,1)S(1)}, u32[]{:S(2)}, u32[]{:S(2)}) async-start(bf16[4,296,256]{2,1,0:T(8,128)(2,1)} %projected.1), calls=%async_computation | async-start | bytes 1212416 | tf_op jit(solution)/shard_map/all_to_all | solution.py:50
  115.0 2.0 %collective-permute-start.5 = (bf16[288,1792]{1,0:T(8,128)(2,1)}, bf16[288,1792]{1,0:T(8,128)(2,1)S(1)}, u32[]{:S(2)}, u32[]{:S(2)}) collective-permute-start(bf16[288,1792]{1,0:T(8,128)(2,1)} %param.19), channel_id=1, source_target_pairs={{0,4},{4,0},{1,5},{5,1},{2,6},{6,2},{3,7},{7,3},{8,12},{12,8},{9,1... | collective-permute-start | bytes 3096584 | tf_op jit(solution)/shard_map/ppermute | solution.py:46
  118.6 7.3 %all-to-all-done = bf16[4,296,256]{2,1,0:T(8,128)(2,1)S(1)} async-done(((bf16[4,296,256]{2,1,0:T(8,128)(2,1)}), bf16[4,296,256]{2,1,0:T(8,128)(2,1)S(1)}, u32[]{:S(2)}, u32[]{:S(2)}) %all-to-all-start) | async-done | bytes 606240 | tf_op jit(solution)/shard_map/all_to_all | solution.py:50
  126.8 3.5 %all-to-all-start.1 = ((bf16[4,2,72,256]{3,2,1,0:T(8,128)(2,1)}), bf16[4,2,72,256]{3,2,1,0:T(8,128)(2,1)S(1)}, u32[]{:S(2)}, u32[]{:S(2)}) async-start(bf16[4,2,72,256]{3,2,1,0:T(8,128)(2,1)} %broadcast_in_dim.125), calls=%async_computation.1 | async-start | bytes 589824 | tf_op jit(solution)/shard_map/all_to_all | solution.py:50
  130.7 6.5 %all-to-all-done.1 = bf16[4,2,72,256]{3,2,1,0:T(8,128)(2,1)S(1)} async-done(((bf16[4,2,72,256]{3,2,1,0:T(8,128)(2,1)}), bf16[4,2,72,256]{3,2,1,0:T(8,128)(2,1)S(1)}, u32[]{:S(2)}, u32[]{:S(2)}) %all-to-all-start.1) | async-done | bytes 294944 | tf_op jit(solution)/shard_map/all_to_all | solution.py:50
  139.1 2.0 collective-permute-start.8
  141.1 3.7 %collective-permute-start.7 = (bf16[8,8,1792]{2,1,0:T(8,128)(2,1)S(1)}, bf16[8,8,1792]{2,1,0:T(8,128)(2,1)S(1)}, u32[]{:S(2)}, u32[]{:S(2)}) collective-permute-start(bf16[8,8,1792]{2,1,0:T(8,128)(2,1)S(1)} %get-tuple-element.22), channel_id=1, source_target_pairs={{0,12},{12,16},{16,28},{28,32},{32,44},{44,48},{48,60},{60,64},{64... | collective-permute-start | bytes 688136 | tf_op jit(solution)/shard_map/ppermute | solution.py:36
  144.8 2.2 %collective-permute-start.6 = (bf16[8,8,1792]{2,1,0:T(8,128)(2,1)S(1)}, bf16[8,8,1792]{2,1,0:T(8,128)(2,1)S(1)}, u32[]{:S(2)}, u32[]{:S(2)}) collective-permute-start(bf16[8,8,1792]{2,1,0:T(8,128)(2,1)S(1)} %get-tuple-element.20), channel_id=1, source_target_pairs={{0,16},{12,28},{16,32},{28,44},{32,48},{44,60},{48,64},{60,76},{64... | collective-permute-start | bytes 688136 | tf_op jit(solution)/shard_map/ppermute | solution.py:36
  147.3 4.5 %collective-permute-done.7 = bf16[8,8,1792]{2,1,0:T(8,128)(2,1)S(1)} collective-permute-done((bf16[8,8,1792]{2,1,0:T(8,128)(2,1)S(1)}, bf16[8,8,1792]{2,1,0:T(8,128)(2,1)S(1)}, u32[]{:S(2)}, u32[]{:S(2)}) %collective-permute-start.7) | collective-permute-done | bytes 229408 | tf_op jit(solution)/shard_map/ppermute | solution.py:36
  151.8 5.3 %collective-permute-done.6 = bf16[8,8,1792]{2,1,0:T(8,128)(2,1)S(1)} collective-permute-done((bf16[8,8,1792]{2,1,0:T(8,128)(2,1)S(1)}, bf16[8,8,1792]{2,1,0:T(8,128)(2,1)S(1)}, u32[]{:S(2)}, u32[]{:S(2)}) %collective-permute-start.6) | collective-permute-done | bytes 229408 | tf_op jit(solution)/shard_map/ppermute | solution.py:36
  157.3 2.0 collective-permute-start.9
  159.3 10.6 %collective-permute-done.9 = bf16[4,8,1792]{2,1,0:T(8,128)(2,1)S(1)} collective-permute-done((bf16[4,8,1792]{2,1,0:T(8,128)(2,1)S(1)}, bf16[4,8,1792]{2,1,0:T(8,128)(2,1)S(1)}, u32[]{:S(2)}, u32[]{:S(2)}) %collective-permute-start.9) | collective-permute-done | bytes 114720 | tf_op jit(solution)/shard_map/ppermute | solution.py:36
  170.5 3.5 %all-to-all-start.2 = ((bf16[4,8,1792]{2,1,0:T(8,128)(2,1)}), bf16[4,8,1792]{2,1,0:T(8,128)(2,1)S(1)}, u32[]{:S(2)}, u32[]{:S(2)}) async-start(bf16[4,8,1792]{2,1,0:T(8,128)(2,1)} %fusion.6), calls=%async_computation.2 | async-start | bytes 229376 | tf_op jit(solution)/shard_map/all_to_all | solution.py:273
  174.1 3.1 %collective-permute-start.4 = (bf16[2,32,640]{2,1,0:T(8,128)(2,1)S(1)}, bf16[2,32,640]{2,1,0:T(8,128)(2,1)S(1)}, u32[]{:S(2)}, u32[]{:S(2)}) collective-permute-start(bf16[2,32,640]{2,1,0:T(8,128)(2,1)S(1)} %get-tuple-element.24), channel_id=1, source_target_pairs={{0,3},{1,0},{2,1},{3,2},{4,7},{5,4},{6,5},{7,6},{8,11},{9,8},{10,9... | collective-permute-start | bytes 245768 | tf_op jit(solution)/shard_map/ppermute | solution.py:119
  177.2 3.4 %collective-permute-start.3 = (bf16[2,32,640]{2,1,0:T(8,128)(2,1)S(1)}, bf16[2,32,640]{2,1,0:T(8,128)(2,1)S(1)}, u32[]{:S(2)}, u32[]{:S(2)}) collective-permute-start(bf16[2,32,640]{2,1,0:T(8,128)(2,1)S(1)} %get-tuple-element.25), channel_id=1, source_target_pairs={{0,2},{1,3},{2,0},{3,1},{4,6},{5,7},{6,4},{7,5},{8,10},{9,11},{10,... | collective-permute-start | bytes 245768 | tf_op jit(solution)/shard_map/ppermute | solution.py:119
  180.7 2.0 collective-permute-start.2
  182.7 2.4 %collective-permute-done.3 = bf16[2,32,640]{2,1,0:T(8,128)(2,1)S(1)} collective-permute-done((bf16[2,32,640]{2,1,0:T(8,128)(2,1)S(1)}, bf16[2,32,640]{2,1,0:T(8,128)(2,1)S(1)}, u32[]{:S(2)}, u32[]{:S(2)}) %collective-permute-start.3) | collective-permute-done | bytes 81952 | tf_op jit(solution)/shard_map/ppermute | solution.py:119
  185.1 3.1 %collective-permute-done.2 = bf16[2,32,640]{2,1,0:T(8,128)(2,1)S(1)} collective-permute-done((bf16[2,32,640]{2,1,0:T(8,128)(2,1)S(1)}, bf16[2,32,640]{2,1,0:T(8,128)(2,1)S(1)}, u32[]{:S(2)}, u32[]{:S(2)}) %collective-permute-start.2) | collective-permute-done | bytes 81952 | tf_op jit(solution)/shard_map/ppermute | solution.py:119
  189.5 9.5 %all-to-all-done.2 = bf16[4,8,1792]{2,1,0:T(8,128)(2,1)S(1)} async-done(((bf16[4,8,1792]{2,1,0:T(8,128)(2,1)}), bf16[4,8,1792]{2,1,0:T(8,128)(2,1)S(1)}, u32[]{:S(2)}, u32[]{:S(2)}) %all-to-all-start.2) | async-done | bytes 114720 | tf_op jit(solution)/shard_map/all_to_all | solution.py:273
  (68 shorter events, 11.3 us)
Async XLA Ops:
  0.6 116.7 %copy-start = (bf16[2,256,512]{2,1,0:T(8,128)(2,1)S(1)}, bf16[2,256,512]{2,1,0:T(8,128)(2,1)}, u32[]{:S(2)}) copy-start(bf16[2,256,512]{2,1,0:T(8,128)(2,1)} %param.12) | copy-start | bytes 1572868
  0.6 101.1 %copy-start.1 = (bf16[1792,288]{0,1:T(8,128)(2,1)S(1)}, bf16[1792,288]{0,1:T(8,128)(2,1)}, u32[]{:S(2)}) copy-start(bf16[1792,288]{0,1:T(8,128)(2,1)} %param.17) | copy-start | bytes 3096580
  0.7 101.0 %collective-permute-start = (bf16[288,1792]{1,0:T(8,128)(2,1)}, bf16[288,1792]{1,0:T(8,128)(2,1)S(1)}, u32[]{:S(2)}, u32[]{:S(2)}) collective-permute-start(bf16[288,1792]{1,0:T(8,128)(2,1)} %bitcast.59), channel_id=1, source_target_pairs={{0,4},{4,0},{1,5},{5,1},{2,6},{6,2},{3,7},{7,3},{8,12},{12,8},{9,1... | collective-permute-start | bytes 3096584 | tf_op jit(solution)/shard_map/ppermute | solution.py:46
  2.7 99.0 %collective-permute-start.1 = (bf16[288,1792]{1,0:T(8,128)(2,1)}, bf16[288,1792]{1,0:T(8,128)(2,1)}, u32[]{:S(2)}, u32[]{:S(2)}) collective-permute-start(bf16[288,1792]{1,0:T(8,128)(2,1)} %bitcast.61), channel_id=1, source_target_pairs={{0,4},{4,0},{1,5},{5,1},{2,6},{6,2},{3,7},{7,3},{8,12},{12,8},{9,1... | collective-permute-start | bytes 3096584 | tf_op jit(solution)/shard_map/ppermute | solution.py:46
  8.9 108.1 %copy-start.6 = (bf16[2,64,256]{2,1,0:T(8,128)(2,1)S(1)}, bf16[2,64,256]{2,1,0:T(8,128)(2,1)}, u32[]{:S(2)}) copy-start(bf16[2,64,256]{2,1,0:T(8,128)(2,1)} %param.13) | copy-start | bytes 196612
  8.9 108.1 %copy-start.7 = (bf16[2,64,128]{2,1,0:T(8,128)(2,1)S(1)}, bf16[2,64,128]{2,1,0:T(8,128)(2,1)}, u32[]{:S(2)}) copy-start(bf16[2,64,128]{2,1,0:T(8,128)(2,1)} %param.11) | copy-start | bytes 98308
  102.9 14.4 %copy-start.4 = (bf16[2,128,512]{2,1,0:T(8,128)(2,1)S(1)}, bf16[2,128,512]{2,1,0:T(8,128)(2,1)}, u32[]{:S(2)}) copy-start(bf16[2,128,512]{2,1,0:T(8,128)(2,1)} %param.10) | copy-start | bytes 786436
  110.4 15.5 %all-to-all-start = ((bf16[4,296,256]{2,1,0:T(8,128)(2,1)}), bf16[4,296,256]{2,1,0:T(8,128)(2,1)S(1)}, u32[]{:S(2)}, u32[]{:S(2)}) async-start(bf16[4,296,256]{2,1,0:T(8,128)(2,1)} %projected.1), calls=%async_computation | async-start | bytes 1212416 | tf_op jit(solution)/shard_map/all_to_all | solution.py:50
  115.0 22.2 %collective-permute-start.5 = (bf16[288,1792]{1,0:T(8,128)(2,1)}, bf16[288,1792]{1,0:T(8,128)(2,1)S(1)}, u32[]{:S(2)}, u32[]{:S(2)}) collective-permute-start(bf16[288,1792]{1,0:T(8,128)(2,1)} %param.19), channel_id=1, source_target_pairs={{0,4},{4,0},{1,5},{5,1},{2,6},{6,2},{3,7},{7,3},{8,12},{12,8},{9,1... | collective-permute-start | bytes 3096584 | tf_op jit(solution)/shard_map/ppermute | solution.py:46
  126.8 10.3 %all-to-all-start.1 = ((bf16[4,2,72,256]{3,2,1,0:T(8,128)(2,1)}), bf16[4,2,72,256]{3,2,1,0:T(8,128)(2,1)S(1)}, u32[]{:S(2)}, u32[]{:S(2)}) async-start(bf16[4,2,72,256]{3,2,1,0:T(8,128)(2,1)} %broadcast_in_dim.125), calls=%async_computation.1 | async-start | bytes 589824 | tf_op jit(solution)/shard_map/all_to_all | solution.py:50
  138.4 8.6 %copy-start.10 = (pred[128]{0:T(512)(128)(4,1)S(1)}, pred[128]{0:T(512)(128)(4,1)}, u32[]{:S(2)}) copy-start(pred[128]{0:T(512)(128)(4,1)} %get-tuple-element.38) | copy-start | bytes 388
  138.4 8.6 %copy-start.11 = (pred[128]{0:T(512)(128)(4,1)S(1)}, pred[128]{0:T(512)(128)(4,1)}, u32[]{:S(2)}) copy-start(pred[128]{0:T(512)(128)(4,1)} %get-tuple-element.39) | copy-start | bytes 388
  138.4 8.6 %copy-start.12 = (pred[128]{0:T(512)(128)(4,1)S(1)}, pred[128]{0:T(512)(128)(4,1)}, u32[]{:S(2)}) copy-start(pred[128]{0:T(512)(128)(4,1)} %get-tuple-element.40) | copy-start | bytes 388
  138.4 8.7 %copy-start.13 = (pred[128]{0:T(512)(128)(4,1)S(1)}, pred[128]{0:T(512)(128)(4,1)}, u32[]{:S(2)}) copy-start(pred[128]{0:T(512)(128)(4,1)} %get-tuple-element.41) | copy-start | bytes 388
  138.4 8.7 %copy-start.14 = (pred[128]{0:T(512)(128)(4,1)S(1)}, pred[128]{0:T(512)(128)(4,1)}, u32[]{:S(2)}) copy-start(pred[128]{0:T(512)(128)(4,1)} %get-tuple-element.42) | copy-start | bytes 388
  139.1 8.2 %collective-permute-start.8 = (bf16[8,8,1792]{2,1,0:T(8,128)(2,1)S(1)}, bf16[8,8,1792]{2,1,0:T(8,128)(2,1)S(1)}, u32[]{:S(2)}, u32[]{:S(2)}) collective-permute-start(bf16[8,8,1792]{2,1,0:T(8,128)(2,1)S(1)} %get-tuple-element.21), channel_id=1, source_target_pairs={{0,252},{12,0},{16,12},{28,16},{32,28},{44,32},{48,44},{60,48},{64... | collective-permute-start | bytes 688136 | tf_op jit(solution)/shard_map/ppermute | solution.py:36
  141.1 10.8 %collective-permute-start.7 = (bf16[8,8,1792]{2,1,0:T(8,128)(2,1)S(1)}, bf16[8,8,1792]{2,1,0:T(8,128)(2,1)S(1)}, u32[]{:S(2)}, u32[]{:S(2)}) collective-permute-start(bf16[8,8,1792]{2,1,0:T(8,128)(2,1)S(1)} %get-tuple-element.22), channel_id=1, source_target_pairs={{0,12},{12,16},{16,28},{28,32},{32,44},{44,48},{48,60},{60,64},{64... | collective-permute-start | bytes 688136 | tf_op jit(solution)/shard_map/ppermute | solution.py:36
  144.8 12.4 %collective-permute-start.6 = (bf16[8,8,1792]{2,1,0:T(8,128)(2,1)S(1)}, bf16[8,8,1792]{2,1,0:T(8,128)(2,1)S(1)}, u32[]{:S(2)}, u32[]{:S(2)}) collective-permute-start(bf16[8,8,1792]{2,1,0:T(8,128)(2,1)S(1)} %get-tuple-element.20), channel_id=1, source_target_pairs={{0,16},{12,28},{16,32},{28,44},{32,48},{44,60},{48,64},{60,76},{64... | collective-permute-start | bytes 688136 | tf_op jit(solution)/shard_map/ppermute | solution.py:36
  157.3 12.6 %collective-permute-start.9 = (bf16[4,8,1792]{2,1,0:T(8,128)(2,1)S(1)}, bf16[4,8,1792]{2,1,0:T(8,128)(2,1)S(1)}, u32[]{:S(2)}, u32[]{:S(2)}) collective-permute-start(bf16[4,8,1792]{2,1,0:T(8,128)(2,1)S(1)} %dynamic-slice_bitcast_fusion.3), channel_id=1, source_target_pairs={{0,32},{12,44},{16,48},{28,60},{32,64},{44,76},{48,80},{60,92},{64... | collective-permute-start | bytes 344072 | tf_op jit(solution)/shard_map/ppermute | solution.py:36
  170.5 28.4 %copy-start.5 = (bf16[8,1792]{1,0:T(8,128)(2,1)S(1)}, bf16[8,1792]{1,0:T(8,128)(2,1)}, u32[]{:S(2)}) copy-start(bf16[8,1792]{1,0:T(8,128)(2,1)} %param.15) | copy-start | bytes 86020
  170.5 28.4 %all-to-all-start.2 = ((bf16[4,8,1792]{2,1,0:T(8,128)(2,1)}), bf16[4,8,1792]{2,1,0:T(8,128)(2,1)S(1)}, u32[]{:S(2)}, u32[]{:S(2)}) async-start(bf16[4,8,1792]{2,1,0:T(8,128)(2,1)} %fusion.6), calls=%async_computation.2 | async-start | bytes 229376 | tf_op jit(solution)/shard_map/all_to_all | solution.py:273
  174.1 8.5 %collective-permute-start.4 = (bf16[2,32,640]{2,1,0:T(8,128)(2,1)S(1)}, bf16[2,32,640]{2,1,0:T(8,128)(2,1)S(1)}, u32[]{:S(2)}, u32[]{:S(2)}) collective-permute-start(bf16[2,32,640]{2,1,0:T(8,128)(2,1)S(1)} %get-tuple-element.24), channel_id=1, source_target_pairs={{0,3},{1,0},{2,1},{3,2},{4,7},{5,4},{6,5},{7,6},{8,11},{9,8},{10,9... | collective-permute-start | bytes 245768 | tf_op jit(solution)/shard_map/ppermute | solution.py:119
  177.2 7.9 %collective-permute-start.3 = (bf16[2,32,640]{2,1,0:T(8,128)(2,1)S(1)}, bf16[2,32,640]{2,1,0:T(8,128)(2,1)S(1)}, u32[]{:S(2)}, u32[]{:S(2)}) collective-permute-start(bf16[2,32,640]{2,1,0:T(8,128)(2,1)S(1)} %get-tuple-element.25), channel_id=1, source_target_pairs={{0,2},{1,3},{2,0},{3,1},{4,6},{5,7},{6,4},{7,5},{8,10},{9,11},{10,... | collective-permute-start | bytes 245768 | tf_op jit(solution)/shard_map/ppermute | solution.py:119
  180.7 7.6 %collective-permute-start.2 = (bf16[2,32,640]{2,1,0:T(8,128)(2,1)S(1)}, bf16[2,32,640]{2,1,0:T(8,128)(2,1)S(1)}, u32[]{:S(2)}, u32[]{:S(2)}) collective-permute-start(bf16[2,32,640]{2,1,0:T(8,128)(2,1)S(1)} %get-tuple-element.26), channel_id=1, source_target_pairs={{0,1},{1,2},{2,3},{3,0},{4,5},{5,6},{6,7},{7,4},{8,9},{9,10},{10,1... | collective-permute-start | bytes 245768 | tf_op jit(solution)/shard_map/ppermute | solution.py:119
  (4 other events, 19.1 us)

commit v2 on v1

--- a/solution.py
+++ b/solution.py
@@ -60,11 +60,9 @@
 
 
 def with_columns(x, columns):
-    lane = lax.broadcasted_iota(jnp.int32, (*(1,) * (x.ndim - 1), 128), x.ndim - 1)
-    extra = jnp.zeros((*x.shape[:-1], 128), jnp.float32)
-    for k, column in enumerate(columns):
-        extra = jnp.where(lane == k, column[..., None], extra)
-    return jnp.concatenate([x.astype(jnp.bfloat16), extra.astype(jnp.bfloat16)], axis=-1)
+    extra = jnp.stack(columns, axis=-1).astype(jnp.bfloat16)
+    extra = jnp.pad(extra, [(0, 0)] * (x.ndim - 1) + [(0, 128 - len(columns))])
+    return jnp.concatenate([x.astype(jnp.bfloat16), extra], axis=-1)
 
 
 def local_partials(
@@ -140,51 +138,51 @@
         return lax.dynamic_index_in_dim(blocks, k, 1, keepdims=False)
 
     half = window // 2
-    arrived = [along_lane(block(partial, (place + half) % window), half, -half)]
+    sends = [((place + half) % window, half, -half)]
     for hops in range(half - 1, 0, -1):
-        arrived += [
-            along_lane(block(partial, (place + hops) % window), hops, hops),
-            along_lane(block(partial, (place + window - hops) % window), -hops, -hops),
-        ]
+        sends += [((place + hops) % window, hops, hops)]
+        sends += [((place + window - hops) % window, -hops, -hops)]
+    blocks = [block(partial, send[0]) for send in sends]
+    arrived = [along_lane(b, *send[1:]) for b, send in zip(blocks, sends)]
     total = block(partial, place).astype(jnp.float32)
     for other in arrived:
         total = total + other.astype(jnp.float32)
     total = total.astype(jnp.bfloat16).reshape(far, 2, *partial.shape[2:])
-    other = along_lane(block(total, 1 - side), window, -window)
+    sent = block(total, 1 - side)
+    other = along_lane(sent, window, -window)
     total = block(total, side).astype(jnp.float32) + other.astype(jnp.float32)
     return total.astype(jnp.bfloat16)
 
 
 def project_kernel(x_ref, gain_ref, *refs):
     *w_refs, out_ref, w_vmem, arrived = refs
+    units = w_refs[0].shape[0]
     copies = [
-        pltpu.make_async_copy(w_ref, w_vmem.at[k], arrived.at[k]) for k, w_ref in enumerate(w_refs)
+        pltpu.make_async_copy(w_ref, w_vmem.at[pl.ds(k * units, units)], arrived.at[k])
+        for k, w_ref in enumerate(w_refs)
     ]
     for copy in copies:
         copy.start()
-    cols, _, _ = out_ref.shape
-    share = w_vmem.shape[1] // cols
+    cols, _, tokens = out_ref.shape
+    share = units // cols
     x = x_ref[...].astype(jnp.float32)
     scaled = (x * gain_ref[...].astype(jnp.float32)).astype(jnp.bfloat16)
-    squares = lax.dot_general(
-        jnp.ones((8, x.shape[1]), jnp.float32),
-        x * x,
-        (((1,), (1,)), ((), ())),
-        precision=lax.Precision.HIGHEST,
-        preferred_element_type=jnp.float32,
-    )
+    squares = jnp.sum(x * x, axis=1, keepdims=True)
+    squares = jnp.broadcast_to(squares, (tokens, 128)).T[:8]
     coarse = squares.astype(jnp.bfloat16).astype(jnp.float32)
     row = lax.broadcasted_iota(jnp.int32, squares.shape, 0)
     norms = jnp.where(row == 0, coarse, squares - coarse).astype(jnp.bfloat16)
     for c in range(cols):
         out_ref[c, len(copies) * share :, :] = norms
-    for k, copy in enumerate(copies):
+    for copy in copies:
         copy.wait()
-        product = lax.dot_general(
-            w_vmem[k], scaled, (((1,), (1,)), ((), ())), preferred_element_type=jnp.float32
-        ).astype(jnp.bfloat16)
+    product = lax.dot_general(
+        w_vmem[...], scaled, (((1,), (1,)), ((), ())), preferred_element_type=jnp.float32
+    ).astype(jnp.bfloat16)
+    for k in range(len(copies)):
         for c in range(cols):
-            out_ref[c, k * share : (k + 1) * share, :] = product[c * share : (c + 1) * share, :]
+            start = k * units + c * share
+            out_ref[c, k * share : (k + 1) * share, :] = product[start : start + share, :]
 
 
 def projected(gathered, gain, weights, cols):
@@ -198,7 +196,7 @@
         in_specs=[whole, whole] + [pl.BlockSpec(memory_space=pltpu.HBM)] * len(weights),
         out_specs=whole,
         scratch_shapes=[
-            pltpu.VMEM((len(weights), units, width), jnp.bfloat16),
+            pltpu.VMEM((len(weights) * units, width), jnp.bfloat16),
             pltpu.SemaphoreType.DMA((len(weights),)),
         ],
         compiler_params=pltpu.CompilerParams(vmem_limit_bytes=24 << 20),
@@ -208,7 +206,7 @@
             transcendentals=0,
         ),
         name="projected",
-    )(gathered, gain[None, :], *weights)
+    )(gathered, gain, *weights)
 
 
 def feed_forward(ffn_rows, norm_gain, w_gate, w_up, w_down, queries):
@@ -264,10 +262,11 @@
         w_gate,
         w_up,
         w_down,
-        (compressed_absorbed_queries, query_rope),
-    )
+        (compressed_absorbed_queries, query_rope, cache_rope, seq_lengths, column),
+    )
+    queries, query_rope, cache_rope, seq_lengths, position = queries
     packed = packed_attention(
-        *queries, compressed_stored_keys, cache_rope, seq_lengths, column
+        queries, query_rope, compressed_stored_keys, cache_rope, seq_lengths, position
     )
     near = summed_near(partial)
     pieces = lax.all_to_all(row_major(near), FAR, 0, 0, tiled=True)

time: 200 us -> 197 us (0.985)
  Pallas kernels: 7.47 us -> 4.73 us
  other arithmetic: 6.39 us -> 3.9 us
    pallas_call x1, Pallas kernels: 7.47 us -> 4.73 us  [projected(): pl.pallas_call(project_kernel, out_shape=jax.ShapeDtypeStruct((cols, rows...]
  transfers between devices with their start and end apart: 13 -> 13, of which waited for: 8 -> 8; matrix products, arithmetic and copies ran while one was open for 4% -> 1% of each run, Pallas kernels for 0% -> 0%
where the time goes in v2:
time: 197 us; the launch traced here: 196 us
  blocking collectives  92.7 us (47%)
  waiting for transfers between devices  50.7 us (26%)
  starting transfers between devices  36.5 us (19%)
  Pallas kernels  4.73 us (2%)
  other arithmetic  3.9 us (2%)
  matrix products  3.16 us (2%)
  local copies, waits for them, and re-layouts  2.92 us (1%)
    all_gather x1, blocking collectives, gathered_on_lane(): return lax.all_gather(x, ROW, axis_index_groups=lanes, axis=0, tiled=True)  92.7 us
    ppermute x4, waiting for transfers between devices, along_lane(): return lax.ppermute(x, ROW, pairs)  20.5 us
    all_to_all x2, waiting for transfers between devices, exchanged(): return lax.all_to_all(pieces, COL, split_axis=0, concat_axis=0, tiled=True)  15.2 us
    ppermute x4, starting transfers between devices, along_lane(): return lax.ppermute(x, ROW, pairs)  9.76 us
    all_to_all x1, waiting for transfers between devices, on_device(): pieces = lax.all_to_all(row_major(near), FAR, 0, 0, tiled=True)  9.41 us
    ppermute x3, starting transfers between devices, merged_attention(): piece = lax.ppermute(piece, COL, [(c, (c + k) % cols) for c in range(cols)])  8.48 us
    all_to_all x2, starting transfers between devices, exchanged(): return lax.all_to_all(pieces, COL, split_axis=0, concat_axis=0, tiled=True)  8.13 us
    ppermute x3, starting transfers between devices, swapped(): return lax.ppermute(x, CORE, [(0, 1), (1, 0)])  6.58 us
  transfers between devices with their start and end apart: 13, of which 8 were waited for; matrix products, arithmetic and copies ran while one was open for 1% of the time, Pallas kernels for 0%

profile of v2, /device:TPU:40, one launch (start us, length us, event | category | flops | bytes accessed | tf_op | source)
XLA Modules:
  0.0 195.7 jit_solution(1011772131434968776)
XLA Ops:
  0.7 2.1 %collective-permute-start = (bf16[288,1792]{1,0:T(8,128)(2,1)}, bf16[288,1792]{1,0:T(8,128)(2,1)S(1)}, u32[]{:S(2)}, u32[]{:S(2)}) collective-permute-start(bf16[288,1792]{1,0:T(8,128)(2,1)} %bitcast.85), channel_id=1, source_target_pairs={{0,4},{4,0},{1,5},{5,1},{2,6},{6,2},{3,7},{7,3},{8,12},{12,8},{9,1... | collective-permute-start | bytes 3096584 | tf_op jit(solution)/shard_map/ppermute | solution.py:46
  2.7 2.4 %collective-permute-start.1 = (bf16[288,1792]{1,0:T(8,128)(2,1)}, bf16[288,1792]{1,0:T(8,128)(2,1)}, u32[]{:S(2)}, u32[]{:S(2)}) collective-permute-start(bf16[288,1792]{1,0:T(8,128)(2,1)} %bitcast.87), channel_id=1, source_target_pairs={{0,4},{4,0},{1,5},{5,1},{2,6},{6,2},{3,7},{7,3},{8,12},{12,8},{9,1... | collective-permute-start | bytes 3096584 | tf_op jit(solution)/shard_map/ppermute | solution.py:46
  5.4 92.7 %all_gather.3.x_ref = bf16[256,1792]{1,0:T(8,128)(2,1)S(1)} all-gather(bf16[8,1792]{1,0:T(8,128)(2,1)} %param.15), channel_id=1, replica_groups={{0,12,16,28,32,44,48,60,64,76,80,92,96,108,112,124,128,140,144,156,160,..., dimensions={0}, use_global_device_ids=true | all-gather | bytes 946176 | tf_op jit(solution)/shard_map/all_gather | solution.py:42
  99.9 4.7 %projected.1 = bf16[4,296,256]{2,1,0:T(8,128)(2,1)} custom-call(bf16[256,1792]{1,0:T(8,128)(2,1)S(1)} %all_gather.3.x_ref, bf16[1792]{0:T(1024)(128)(2,1)S(1)} %copy-done.3, bf16[288,1792]{1,0:T(8,128)(2,1)S(1)} %bitcast.86, bf16[288,1792]{1,0:T(8,128)(2,1)S(1)} %bitcast.88, bf16[288,1792]{1,0:T(8,128)(2,1)S(1)} %collective-permute-done.refs_2_, ...), custom_call_target="tpu_custom_call" | custom-call | flops 1056964608 | bytes 4128768 | tf_op jit(solution)/shard_map/projected/pallas_call | solution.py:193
  105.7 1.3 fusion.51
  107.1 4.6 %all-to-all-start = ((bf16[4,296,256]{2,1,0:T(8,128)(2,1)}), bf16[4,296,256]{2,1,0:T(8,128)(2,1)S(1)}, u32[]{:S(2)}, u32[]{:S(2)}) async-start(bf16[4,296,256]{2,1,0:T(8,128)(2,1)} %projected.1), calls=%async_computation | async-start | bytes 1212416 | tf_op jit(solution)/shard_map/all_to_all | solution.py:50
  111.9 2.1 %collective-permute-start.5 = (bf16[288,1792]{1,0:T(8,128)(2,1)S(1)}, bf16[288,1792]{1,0:T(8,128)(2,1)S(1)}, u32[]{:S(2)}, u32[]{:S(2)}) collective-permute-start(bf16[288,1792]{1,0:T(8,128)(2,1)S(1)} %copy-done.4), channel_id=1, source_target_pairs={{0,4},{4,0},{1,5},{5,1},{2,6},{6,2},{3,7},{7,3},{8,12},{12,8},{9,1... | collective-permute-start | bytes 3096584 | tf_op jit(solution)/shard_map/ppermute | solution.py:46
  114.0 8.6 %all-to-all-done = bf16[4,296,256]{2,1,0:T(8,128)(2,1)S(1)} async-done(((bf16[4,296,256]{2,1,0:T(8,128)(2,1)}), bf16[4,296,256]{2,1,0:T(8,128)(2,1)S(1)}, u32[]{:S(2)}, u32[]{:S(2)}) %all-to-all-start) | async-done | bytes 606240 | tf_op jit(solution)/shard_map/all_to_all | solution.py:50
  123.5 3.5 %all-to-all-start.1 = ((bf16[4,2,72,256]{3,2,1,0:T(8,128)(2,1)}), bf16[4,2,72,256]{3,2,1,0:T(8,128)(2,1)S(1)}, u32[]{:S(2)}, u32[]{:S(2)}) async-start(bf16[4,2,72,256]{3,2,1,0:T(8,128)(2,1)} %broadcast_in_dim.33), calls=%async_computation.1 | async-start | bytes 589824 | tf_op jit(solution)/shard_map/all_to_all | solution.py:50
  127.3 6.6 %all-to-all-done.1 = bf16[4,2,72,256]{3,2,1,0:T(8,128)(2,1)S(1)} async-done(((bf16[4,2,72,256]{3,2,1,0:T(8,128)(2,1)}), bf16[4,2,72,256]{3,2,1,0:T(8,128)(2,1)S(1)}, u32[]{:S(2)}, u32[]{:S(2)}) %all-to-all-start.1) | async-done | bytes 294944 | tf_op jit(solution)/shard_map/all_to_all | solution.py:50
  135.3 2.0 collective-permute-start.8
  137.2 3.7 %collective-permute-start.7 = (bf16[8,8,1792]{2,1,0:T(8,128)(2,1)S(1)}, bf16[8,8,1792]{2,1,0:T(8,128)(2,1)S(1)}, u32[]{:S(2)}, u32[]{:S(2)}) collective-permute-start(bf16[8,8,1792]{2,1,0:T(8,128)(2,1)S(1)} %get-tuple-element.28), channel_id=1, source_target_pairs={{0,12},{12,16},{16,28},{28,32},{32,44},{44,48},{48,60},{60,64},{64... | collective-permute-start | bytes 688136 | tf_op jit(solution)/shard_map/ppermute | solution.py:36
  140.9 2.2 %collective-permute-start.6 = (bf16[8,8,1792]{2,1,0:T(8,128)(2,1)S(1)}, bf16[8,8,1792]{2,1,0:T(8,128)(2,1)S(1)}, u32[]{:S(2)}, u32[]{:S(2)}) collective-permute-start(bf16[8,8,1792]{2,1,0:T(8,128)(2,1)S(1)} %get-tuple-element.26), channel_id=1, source_target_pairs={{0,16},{12,28},{16,32},{28,44},{32,48},{44,60},{48,64},{60,76},{64... | collective-permute-start | bytes 688136 | tf_op jit(solution)/shard_map/ppermute | solution.py:36
  143.4 4.6 %collective-permute-done.7 = bf16[8,8,1792]{2,1,0:T(8,128)(2,1)S(1)} collective-permute-done((bf16[8,8,1792]{2,1,0:T(8,128)(2,1)S(1)}, bf16[8,8,1792]{2,1,0:T(8,128)(2,1)S(1)}, u32[]{:S(2)}, u32[]{:S(2)}) %collective-permute-start.7) | collective-permute-done | bytes 229408 | tf_op jit(solution)/shard_map/ppermute | solution.py:36
  148.0 5.3 %collective-permute-done.6 = bf16[8,8,1792]{2,1,0:T(8,128)(2,1)S(1)} collective-permute-done((bf16[8,8,1792]{2,1,0:T(8,128)(2,1)S(1)}, bf16[8,8,1792]{2,1,0:T(8,128)(2,1)S(1)}, u32[]{:S(2)}, u32[]{:S(2)}) %collective-permute-start.6) | collective-permute-done | bytes 229408 | tf_op jit(solution)/shard_map/ppermute | solution.py:36
  153.4 2.0 collective-permute-start.9
  155.4 10.6 %collective-permute-done.9 = bf16[4,8,1792]{2,1,0:T(8,128)(2,1)S(1)} collective-permute-done((bf16[4,8,1792]{2,1,0:T(8,128)(2,1)S(1)}, bf16[4,8,1792]{2,1,0:T(8,128)(2,1)S(1)}, u32[]{:S(2)}, u32[]{:S(2)}) %collective-permute-start.9) | collective-permute-done | bytes 114720 | tf_op jit(solution)/shard_map/ppermute | solution.py:36
  166.7 3.5 %all-to-all-start.2 = ((bf16[4,8,1792]{2,1,0:T(8,128)(2,1)}), bf16[4,8,1792]{2,1,0:T(8,128)(2,1)S(1)}, u32[]{:S(2)}, u32[]{:S(2)}) async-start(bf16[4,8,1792]{2,1,0:T(8,128)(2,1)} %fusion.8), calls=%async_computation.2 | async-start | bytes 229376 | tf_op jit(solution)/shard_map/all_to_all | solution.py:272
  170.3 3.1 %collective-permute-start.4 = (bf16[2,32,640]{2,1,0:T(8,128)(2,1)S(1)}, bf16[2,32,640]{2,1,0:T(8,128)(2,1)S(1)}, u32[]{:S(2)}, u32[]{:S(2)}) collective-permute-start(bf16[2,32,640]{2,1,0:T(8,128)(2,1)S(1)} %get-tuple-element.30), channel_id=1, source_target_pairs={{0,3},{1,0},{2,1},{3,2},{4,7},{5,4},{6,5},{7,6},{8,11},{9,8},{10,9... | collective-permute-start | bytes 245768 | tf_op jit(solution)/shard_map/ppermute | solution.py:117
  173.4 3.4 %collective-permute-start.3 = (bf16[2,32,640]{2,1,0:T(8,128)(2,1)S(1)}, bf16[2,32,640]{2,1,0:T(8,128)(2,1)S(1)}, u32[]{:S(2)}, u32[]{:S(2)}) collective-permute-start(bf16[2,32,640]{2,1,0:T(8,128)(2,1)S(1)} %get-tuple-element.31), channel_id=1, source_target_pairs={{0,2},{1,3},{2,0},{3,1},{4,6},{5,7},{6,4},{7,5},{8,10},{9,11},{10,... | collective-permute-start | bytes 245768 | tf_op jit(solution)/shard_map/ppermute | solution.py:117
  176.9 2.0 collective-permute-start.2
  178.8 2.4 %collective-permute-done.3 = bf16[2,32,640]{2,1,0:T(8,128)(2,1)S(1)} collective-permute-done((bf16[2,32,640]{2,1,0:T(8,128)(2,1)S(1)}, bf16[2,32,640]{2,1,0:T(8,128)(2,1)S(1)}, u32[]{:S(2)}, u32[]{:S(2)}) %collective-permute-start.3) | collective-permute-done | bytes 81952 | tf_op jit(solution)/shard_map/ppermute | solution.py:117
  181.3 3.1 %collective-permute-done.2 = bf16[2,32,640]{2,1,0:T(8,128)(2,1)S(1)} collective-permute-done((bf16[2,32,640]{2,1,0:T(8,128)(2,1)S(1)}, bf16[2,32,640]{2,1,0:T(8,128)(2,1)S(1)}, u32[]{:S(2)}, u32[]{:S(2)}) %collective-permute-start.2) | collective-permute-done | bytes 81952 | tf_op jit(solution)/shard_map/ppermute | solution.py:117
  185.6 9.4 %all-to-all-done.2 = bf16[4,8,1792]{2,1,0:T(8,128)(2,1)S(1)} async-done(((bf16[4,8,1792]{2,1,0:T(8,128)(2,1)}), bf16[4,8,1792]{2,1,0:T(8,128)(2,1)S(1)}, u32[]{:S(2)}, u32[]{:S(2)}) %all-to-all-start.2) | async-done | bytes 114720 | tf_op jit(solution)/shard_map/all_to_all | solution.py:272
  (55 shorter events, 8.7 us)
Async XLA Ops:
  0.6 105.1 %copy-start = (bf16[2,256,512]{2,1,0:T(8,128)(2,1)S(1)}, bf16[2,256,512]{2,1,0:T(8,128)(2,1)}, u32[]{:S(2)}) copy-start(bf16[2,256,512]{2,1,0:T(8,128)(2,1)} %param.12) | copy-start | bytes 1572868
  0.6 97.4 %copy-start.1 = (bf16[1792,288]{0,1:T(8,128)(2,1)S(1)}, bf16[1792,288]{0,1:T(8,128)(2,1)}, u32[]{:S(2)}) copy-start(bf16[1792,288]{0,1:T(8,128)(2,1)} %param.17) | copy-start | bytes 3096580
  0.7 97.4 %collective-permute-start = (bf16[288,1792]{1,0:T(8,128)(2,1)}, bf16[288,1792]{1,0:T(8,128)(2,1)S(1)}, u32[]{:S(2)}, u32[]{:S(2)}) collective-permute-start(bf16[288,1792]{1,0:T(8,128)(2,1)} %bitcast.85), channel_id=1, source_target_pairs={{0,4},{4,0},{1,5},{5,1},{2,6},{6,2},{3,7},{7,3},{8,12},{12,8},{9,1... | collective-permute-start | bytes 3096584 | tf_op jit(solution)/shard_map/ppermute | solution.py:46
  2.7 95.3 %collective-permute-start.1 = (bf16[288,1792]{1,0:T(8,128)(2,1)}, bf16[288,1792]{1,0:T(8,128)(2,1)}, u32[]{:S(2)}, u32[]{:S(2)}) collective-permute-start(bf16[288,1792]{1,0:T(8,128)(2,1)} %bitcast.87), channel_id=1, source_target_pairs={{0,4},{4,0},{1,5},{5,1},{2,6},{6,2},{3,7},{7,3},{8,12},{12,8},{9,1... | collective-permute-start | bytes 3096584 | tf_op jit(solution)/shard_map/ppermute | solution.py:46
  5.3 99.4 %copy-start.6 = (bf16[2,64,256]{2,1,0:T(8,128)(2,1)S(1)}, bf16[2,64,256]{2,1,0:T(8,128)(2,1)}, u32[]{:S(2)}) copy-start(bf16[2,64,256]{2,1,0:T(8,128)(2,1)} %param.13) | copy-start | bytes 196612
  5.3 99.4 %copy-start.7 = (bf16[2,64,128]{2,1,0:T(8,128)(2,1)S(1)}, bf16[2,64,128]{2,1,0:T(8,128)(2,1)}, u32[]{:S(2)}) copy-start(bf16[2,64,128]{2,1,0:T(8,128)(2,1)} %param.11) | copy-start | bytes 98308
  98.0 1.2 copy-start.2
  99.3 0.7 copy-start.3
  104.7 7.2 %copy-start.4 = (bf16[288,1792]{1,0:T(8,128)(2,1)S(1)}, bf16[288,1792]{1,0:T(8,128)(2,1)}, u32[]{:S(2)}) copy-start(bf16[288,1792]{1,0:T(8,128)(2,1)} %param.19) | copy-start | bytes 3096580
  107.1 15.5 %all-to-all-start = ((bf16[4,296,256]{2,1,0:T(8,128)(2,1)}), bf16[4,296,256]{2,1,0:T(8,128)(2,1)S(1)}, u32[]{:S(2)}, u32[]{:S(2)}) async-start(bf16[4,296,256]{2,1,0:T(8,128)(2,1)} %projected.1), calls=%async_computation | async-start | bytes 1212416 | tf_op jit(solution)/shard_map/all_to_all | solution.py:50
  111.9 22.0 %collective-permute-start.5 = (bf16[288,1792]{1,0:T(8,128)(2,1)S(1)}, bf16[288,1792]{1,0:T(8,128)(2,1)S(1)}, u32[]{:S(2)}, u32[]{:S(2)}) collective-permute-start(bf16[288,1792]{1,0:T(8,128)(2,1)S(1)} %copy-done.4), channel_id=1, source_target_pairs={{0,4},{4,0},{1,5},{5,1},{2,6},{6,2},{3,7},{7,3},{8,12},{12,8},{9,1... | collective-permute-start | bytes 3096584 | tf_op jit(solution)/shard_map/ppermute | solution.py:46
  123.5 10.3 %all-to-all-start.1 = ((bf16[4,2,72,256]{3,2,1,0:T(8,128)(2,1)}), bf16[4,2,72,256]{3,2,1,0:T(8,128)(2,1)S(1)}, u32[]{:S(2)}, u32[]{:S(2)}) async-start(bf16[4,2,72,256]{3,2,1,0:T(8,128)(2,1)} %broadcast_in_dim.33), calls=%async_computation.1 | async-start | bytes 589824 | tf_op jit(solution)/shard_map/all_to_all | solution.py:50
  135.3 8.1 %collective-permute-start.8 = (bf16[8,8,1792]{2,1,0:T(8,128)(2,1)S(1)}, bf16[8,8,1792]{2,1,0:T(8,128)(2,1)S(1)}, u32[]{:S(2)}, u32[]{:S(2)}) collective-permute-start(bf16[8,8,1792]{2,1,0:T(8,128)(2,1)S(1)} %get-tuple-element.27), channel_id=1, source_target_pairs={{0,252},{12,0},{16,12},{28,16},{32,28},{44,32},{48,44},{60,48},{64... | collective-permute-start | bytes 688136 | tf_op jit(solution)/shard_map/ppermute | solution.py:36
  137.2 10.8 %collective-permute-start.7 = (bf16[8,8,1792]{2,1,0:T(8,128)(2,1)S(1)}, bf16[8,8,1792]{2,1,0:T(8,128)(2,1)S(1)}, u32[]{:S(2)}, u32[]{:S(2)}) collective-permute-start(bf16[8,8,1792]{2,1,0:T(8,128)(2,1)S(1)} %get-tuple-element.28), channel_id=1, source_target_pairs={{0,12},{12,16},{16,28},{28,32},{32,44},{44,48},{48,60},{60,64},{64... | collective-permute-start | bytes 688136 | tf_op jit(solution)/shard_map/ppermute | solution.py:36
  140.9 12.4 %collective-permute-start.6 = (bf16[8,8,1792]{2,1,0:T(8,128)(2,1)S(1)}, bf16[8,8,1792]{2,1,0:T(8,128)(2,1)S(1)}, u32[]{:S(2)}, u32[]{:S(2)}) collective-permute-start(bf16[8,8,1792]{2,1,0:T(8,128)(2,1)S(1)} %get-tuple-element.26), channel_id=1, source_target_pairs={{0,16},{12,28},{16,32},{28,44},{32,48},{44,60},{48,64},{60,76},{64... | collective-permute-start | bytes 688136 | tf_op jit(solution)/shard_map/ppermute | solution.py:36
  153.4 12.6 %collective-permute-start.9 = (bf16[4,8,1792]{2,1,0:T(8,128)(2,1)S(1)}, bf16[4,8,1792]{2,1,0:T(8,128)(2,1)S(1)}, u32[]{:S(2)}, u32[]{:S(2)}) collective-permute-start(bf16[4,8,1792]{2,1,0:T(8,128)(2,1)S(1)} %dynamic-slice_bitcast_fusion.3), channel_id=1, source_target_pairs={{0,32},{12,44},{16,48},{28,60},{32,64},{44,76},{48,80},{60,92},{64... | collective-permute-start | bytes 344072 | tf_op jit(solution)/shard_map/ppermute | solution.py:36
  166.7 28.3 %copy-start.5 = (bf16[8,1792]{1,0:T(8,128)(2,1)S(1)}, bf16[8,1792]{1,0:T(8,128)(2,1)}, u32[]{:S(2)}) copy-start(bf16[8,1792]{1,0:T(8,128)(2,1)} %param.15) | copy-start | bytes 86020
  166.7 28.3 %all-to-all-start.2 = ((bf16[4,8,1792]{2,1,0:T(8,128)(2,1)}), bf16[4,8,1792]{2,1,0:T(8,128)(2,1)S(1)}, u32[]{:S(2)}, u32[]{:S(2)}) async-start(bf16[4,8,1792]{2,1,0:T(8,128)(2,1)} %fusion.8), calls=%async_computation.2 | async-start | bytes 229376 | tf_op jit(solution)/shard_map/all_to_all | solution.py:272
  170.3 8.5 %collective-permute-start.4 = (bf16[2,32,640]{2,1,0:T(8,128)(2,1)S(1)}, bf16[2,32,640]{2,1,0:T(8,128)(2,1)S(1)}, u32[]{:S(2)}, u32[]{:S(2)}) collective-permute-start(bf16[2,32,640]{2,1,0:T(8,128)(2,1)S(1)} %get-tuple-element.30), channel_id=1, source_target_pairs={{0,3},{1,0},{2,1},{3,2},{4,7},{5,4},{6,5},{7,6},{8,11},{9,8},{10,9... | collective-permute-start | bytes 245768 | tf_op jit(solution)/shard_map/ppermute | solution.py:117
  173.4 7.9 %collective-permute-start.3 = (bf16[2,32,640]{2,1,0:T(8,128)(2,1)S(1)}, bf16[2,32,640]{2,1,0:T(8,128)(2,1)S(1)}, u32[]{:S(2)}, u32[]{:S(2)}) collective-permute-start(bf16[2,32,640]{2,1,0:T(8,128)(2,1)S(1)} %get-tuple-element.31), channel_id=1, source_target_pairs={{0,2},{1,3},{2,0},{3,1},{4,6},{5,7},{6,4},{7,5},{8,10},{9,11},{10,... | collective-permute-start | bytes 245768 | tf_op jit(solution)/shard_map/ppermute | solution.py:117
  176.9 7.6 %collective-permute-start.2 = (bf16[2,32,640]{2,1,0:T(8,128)(2,1)S(1)}, bf16[2,32,640]{2,1,0:T(8,128)(2,1)S(1)}, u32[]{:S(2)}, u32[]{:S(2)}) collective-permute-start(bf16[2,32,640]{2,1,0:T(8,128)(2,1)S(1)} %get-tuple-element.32), channel_id=1, source_target_pairs={{0,1},{1,2},{2,3},{3,0},{4,5},{5,6},{6,7},{7,4},{8,9},{9,10},{10,1... | collective-permute-start | bytes 245768 | tf_op jit(solution)/shard_map/ppermute | solution.py:117

commit v3 on v2

--- a/solution.py
+++ b/solution.py
@@ -108,22 +108,14 @@
     return jnp.moveaxis(packed.reshape(seqs, cols, heads // cols, -1), 1, 0)
 
 
-def merged_attention(packed, latent, column):
-    cols = lax.axis_size(COL)
-    merged = []
-    for k in range(cols):
-        piece = lax.dynamic_index_in_dim(packed, (column + k) % cols, 0, keepdims=False)
-        if k:
-            piece = lax.ppermute(piece, COL, [(c, (c + k) % cols) for c in range(cols)])
-        merged.append(piece.astype(jnp.float32))
-    tops = [m[..., latent] + (m[..., latent + 1] + m[..., latent + 2]) for m in merged]
-    totals = [m[..., latent + 3] + (m[..., latent + 4] + m[..., latent + 5]) for m in merged]
-    top = tops[0]
-    for other in tops[1:]:
-        top = jnp.maximum(top, other)
-    factors = [jnp.exp(t - top) for t in tops]
-    total = sum(t * f for t, f in zip(totals, factors))
-    context = sum(m[..., :latent] * f[..., None] for m, f in zip(merged, factors))
+def merged_attention(packed, latent):
+    merged = exchanged(row_major(packed))
+    merged = merged.astype(jnp.float32)
+    tops = merged[..., latent] + (merged[..., latent + 1] + merged[..., latent + 2])
+    totals = merged[..., latent + 3] + (merged[..., latent + 4] + merged[..., latent + 5])
+    factor = jnp.exp(tops - jnp.max(tops, axis=0, keepdims=True))
+    total = jnp.sum(totals * factor, axis=0)
+    context = jnp.sum(merged[..., :latent] * factor[..., None], axis=0)
     return (context / total[..., None]).astype(jnp.bfloat16)
 
 
@@ -228,7 +220,8 @@
     total = (total[: 4 * share] * scale).reshape(2, 2, share, -1)
     hidden = (jax.nn.silu(total[:, 0]) * total[:, 1]).astype(jnp.bfloat16)
 
-    hidden = exchanged(row_major(jnp.broadcast_to(hidden, (cols, *hidden.shape))))
+    hidden = row_major(jnp.broadcast_to(hidden, (cols, *hidden.shape)))
+    hidden = exchanged(hidden)
     partial = sum(
         lax.dot_general(
             hidden[:, k].reshape(units, -1),
@@ -271,7 +264,7 @@
     near = summed_near(partial)
     pieces = lax.all_to_all(row_major(near), FAR, 0, 0, tiled=True)
     reduced = jnp.sum(pieces.astype(jnp.float32), axis=0)
-    context = merged_attention(packed, compressed_stored_keys.shape[-1], column)
+    context = merged_attention(packed, compressed_stored_keys.shape[-1])
     ffn_out = (ffn_rows.astype(jnp.float32) + reduced).astype(jnp.bfloat16)
     return (context, ffn_out)
 

time: 197 us -> 195 us (0.990)
  starting transfers between devices: 36.5 us -> 31.4 us
  waiting for transfers between devices: 50.7 us -> 55 us
    all_to_all x1, waiting for transfers between devices: 9.41 us -> 23.5 us  [on_device(): pieces = lax.all_to_all(row_major(near), FAR, 0, 0, tiled=True)]
    ppermute x3 -> x0, starting transfers between devices: 8.48 us -> none  [merged_attention(): piece = lax.ppermute(piece, COL, [(c, (c + k) % cols) for c in range(cols)])]
    ppermute x3 -> x0, waiting for transfers between devices: 5.57 us -> none  [merged_attention(): piece = lax.ppermute(piece, COL, [(c, (c + k) % cols) for c in range(cols)])]
    ppermute x4, waiting for transfers between devices: 20.5 us -> 16.2 us  [along_lane(): return lax.ppermute(x, ROW, pairs)]
    all_to_all x2 -> x3, starting transfers between devices: 8.13 us -> 11.7 us  [exchanged(): return lax.all_to_all(pieces, COL, split_axis=0, concat_axis=0, tiled=True)]
    all_to_all x2 -> x3, waiting for transfers between devices: 15.2 us -> 15.3 us  [exchanged(): return lax.all_to_all(pieces, COL, split_axis=0, concat_axis=0, tiled=True)]
  transfers between devices with their start and end apart: 13 -> 11, of which waited for: 8 -> 6; matrix products, arithmetic and copies ran while one was open for 1% -> 2% of each run, Pallas kernels for 0% -> 0%
where the time goes in v3:
time: 195 us
  blocking collectives  92.8 us (48%)
  waiting for transfers between devices  55 us (28%)
  starting transfers between devices  31.4 us (16%)
  local copies, waits for them, and re-layouts  4.88 us (3%)
  Pallas kernels  4.01 us (2%)
  other arithmetic  3.37 us (2%)
  matrix products  2.21 us (1%)
    all_gather x1, blocking collectives, gathered_on_lane(): return lax.all_gather(x, ROW, axis_index_groups=lanes, axis=0, tiled=True)  92.8 us
    all_to_all x1, waiting for transfers between devices, on_device(): pieces = lax.all_to_all(row_major(near), FAR, 0, 0, tiled=True)  23.5 us
    ppermute x4, waiting for transfers between devices, along_lane(): return lax.ppermute(x, ROW, pairs)  16.2 us
    all_to_all x3, waiting for transfers between devices, exchanged(): return lax.all_to_all(pieces, COL, split_axis=0, concat_axis=0, tiled=True)  15.3 us
    all_to_all x3, starting transfers between devices, exchanged(): return lax.all_to_all(pieces, COL, split_axis=0, concat_axis=0, tiled=True)  11.7 us
    ppermute x4, starting transfers between devices, along_lane(): return lax.ppermute(x, ROW, pairs)  9.77 us
    ppermute x3, starting transfers between devices, swapped(): return lax.ppermute(x, CORE, [(0, 1), (1, 0)])  6.55 us
    pallas_call x1, Pallas kernels, projected(): pl.pallas_call(project_kernel, out_shape=jax.ShapeDtypeStruct((cols, rows...  4.01 us
  transfers between devices with their start and end apart: 11, of which 6 were waited for; matrix products, arithmetic and copies ran while one was open for 2% of the time, Pallas kernels for 0%

profile of v3, /device:TPU:40, one launch (start us, length us, event | category | flops | bytes accessed | tf_op | source)
XLA Modules:
  0.0 194.7 jit_solution(6618143225095190791)
XLA Ops:
  0.6 2.1 %collective-permute-start = (bf16[288,1792]{1,0:T(8,128)(2,1)}, bf16[288,1792]{1,0:T(8,128)(2,1)S(1)}, u32[]{:S(2)}, u32[]{:S(2)}) collective-permute-start(bf16[288,1792]{1,0:T(8,128)(2,1)} %bitcast.77), channel_id=1, source_target_pairs={{0,4},{4,0},{1,5},{5,1},{2,6},{6,2},{3,7},{7,3},{8,12},{12,8},{9,1... | collective-permute-start | bytes 3096584 | tf_op jit(solution)/shard_map/ppermute | solution.py:46
  2.7 2.4 %collective-permute-start.1 = (bf16[288,1792]{1,0:T(8,128)(2,1)}, bf16[288,1792]{1,0:T(8,128)(2,1)S(1)}, u32[]{:S(2)}, u32[]{:S(2)}) collective-permute-start(bf16[288,1792]{1,0:T(8,128)(2,1)} %bitcast.79), channel_id=1, source_target_pairs={{0,4},{4,0},{1,5},{5,1},{2,6},{6,2},{3,7},{7,3},{8,12},{12,8},{9,1... | collective-permute-start | bytes 3096584 | tf_op jit(solution)/shard_map/ppermute | solution.py:46
  5.3 92.8 %all_gather.3.x_ref = bf16[256,1792]{1,0:T(8,128)(2,1)S(1)} all-gather(bf16[8,1792]{1,0:T(8,128)(2,1)} %param.15), channel_id=1, replica_groups={{0,12,16,28,32,44,48,60,64,76,80,92,96,108,112,124,128,140,144,156,160,..., dimensions={0}, use_global_device_ids=true | all-gather | bytes 946176 | tf_op jit(solution)/shard_map/all_gather | solution.py:42
  98.1 1.2 copy-done.1
  99.3 1.2 copy-done.2
  100.6 0.7 copy-done.3
  101.2 4.0 %projected.1 = bf16[4,296,256]{2,1,0:T(8,128)(2,1)} custom-call(bf16[256,1792]{1,0:T(8,128)(2,1)S(1)} %all_gather.3.x_ref, bf16[1792]{0:T(1024)(128)(2,1)S(1)} %copy-done.3, bf16[288,1792]{1,0:T(8,128)(2,1)S(1)} %bitcast.78, bf16[288,1792]{1,0:T(8,128)(2,1)S(1)} %bitcast.80, bf16[288,1792]{1,0:T(8,128)(2,1)S(1)} %collective-permute-done.refs_2_, ...), custom_call_target="tpu_custom_call" | custom-call | flops 1056964608 | bytes 4128768 | tf_op jit(solution)/shard_map/projected/pallas_call | solution.py:185
  106.2 4.6 %all-to-all-start.1 = ((bf16[4,296,256]{2,1,0:T(8,128)(2,1)}), bf16[4,296,256]{2,1,0:T(8,128)(2,1)S(1)}, u32[]{:S(2)}, u32[]{:S(2)}) async-start(bf16[4,296,256]{2,1,0:T(8,128)(2,1)} %projected.1), calls=%async_computation.1 | async-start | bytes 1212416 | tf_op jit(solution)/shard_map/all_to_all | solution.py:50
  110.8 2.0 %collective-permute-start.2 = (bf16[288,1792]{1,0:T(8,128)(2,1)}, bf16[288,1792]{1,0:T(8,128)(2,1)S(1)}, u32[]{:S(2)}, u32[]{:S(2)}) collective-permute-start(bf16[288,1792]{1,0:T(8,128)(2,1)} %param.19), channel_id=1, source_target_pairs={{0,4},{4,0},{1,5},{5,1},{2,6},{6,2},{3,7},{7,3},{8,12},{12,8},{9,1... | collective-permute-start | bytes 3096584 | tf_op jit(solution)/shard_map/ppermute | solution.py:46
  113.2 8.6 %all-to-all-done.1 = bf16[4,296,256]{2,1,0:T(8,128)(2,1)S(1)} async-done(((bf16[4,296,256]{2,1,0:T(8,128)(2,1)}), bf16[4,296,256]{2,1,0:T(8,128)(2,1)S(1)}, u32[]{:S(2)}, u32[]{:S(2)}) %all-to-all-start.1) | async-done | bytes 606240 | tf_op jit(solution)/shard_map/all_to_all | solution.py:50
  121.9 0.7 broadcast_in_dim.31
  122.6 3.5 %all-to-all-start.2 = ((bf16[4,2,72,256]{3,2,1,0:T(8,128)(2,1)}), bf16[4,2,72,256]{3,2,1,0:T(8,128)(2,1)S(1)}, u32[]{:S(2)}, u32[]{:S(2)}) async-start(bf16[4,2,72,256]{3,2,1,0:T(8,128)(2,1)} %broadcast_in_dim.31), calls=%async_computation.2 | async-start | bytes 589824 | tf_op jit(solution)/shard_map/all_to_all | solution.py:50
  126.2 6.7 %all-to-all-done.2 = bf16[4,2,72,256]{3,2,1,0:T(8,128)(2,1)S(1)} async-done(((bf16[4,2,72,256]{3,2,1,0:T(8,128)(2,1)}), bf16[4,2,72,256]{3,2,1,0:T(8,128)(2,1)S(1)}, u32[]{:S(2)}, u32[]{:S(2)}) %all-to-all-start.2) | async-done | bytes 294944 | tf_op jit(solution)/shard_map/all_to_all | solution.py:50
  134.4 2.0 %collective-permute-start.5 = (bf16[8,8,1792]{2,1,0:T(8,128)(2,1)S(1)}, bf16[8,8,1792]{2,1,0:T(8,128)(2,1)S(1)}, u32[]{:S(2)}, u32[]{:S(2)}) collective-permute-start(bf16[8,8,1792]{2,1,0:T(8,128)(2,1)S(1)} %get-tuple-element.21), channel_id=1, source_target_pairs={{0,252},{12,0},{16,12},{28,16},{32,28},{44,32},{48,44},{60,48},{64... | collective-permute-start | bytes 688136 | tf_op jit(solution)/shard_map/ppermute | solution.py:36
  136.4 3.7 %collective-permute-start.4 = (bf16[8,8,1792]{2,1,0:T(8,128)(2,1)S(1)}, bf16[8,8,1792]{2,1,0:T(8,128)(2,1)S(1)}, u32[]{:S(2)}, u32[]{:S(2)}) collective-permute-start(bf16[8,8,1792]{2,1,0:T(8,128)(2,1)S(1)} %get-tuple-element.22), channel_id=1, source_target_pairs={{0,12},{12,16},{16,28},{28,32},{32,44},{44,48},{48,60},{60,64},{64... | collective-permute-start | bytes 688136 | tf_op jit(solution)/shard_map/ppermute | solution.py:36
  140.0 2.2 %collective-permute-start.3 = (bf16[8,8,1792]{2,1,0:T(8,128)(2,1)S(1)}, bf16[8,8,1792]{2,1,0:T(8,128)(2,1)S(1)}, u32[]{:S(2)}, u32[]{:S(2)}) collective-permute-start(bf16[8,8,1792]{2,1,0:T(8,128)(2,1)S(1)} %get-tuple-element.20), channel_id=1, source_target_pairs={{0,16},{12,28},{16,32},{28,44},{32,48},{44,60},{48,64},{60,76},{64... | collective-permute-start | bytes 688136 | tf_op jit(solution)/shard_map/ppermute | solution.py:36
  142.4 0.7 copy.40
  143.2 3.5 %all-to-all-start = ((bf16[4,2,32,640]{3,2,1,0:T(8,128)(2,1)}), bf16[4,2,32,640]{3,2,1,0:T(8,128)(2,1)S(1)}, u32[]{:S(2)}, u32[]{:S(2)}) async-start(bf16[4,2,32,640]{3,2,1,0:T(8,128)(2,1)} %bitcast.76), calls=%async_computation | async-start | bytes 655360 | tf_op jit(solution)/shard_map/all_to_all | solution.py:50
  147.1 5.3 %collective-permute-done.3 = bf16[8,8,1792]{2,1,0:T(8,128)(2,1)S(1)} collective-permute-done((bf16[8,8,1792]{2,1,0:T(8,128)(2,1)S(1)}, bf16[8,8,1792]{2,1,0:T(8,128)(2,1)S(1)}, u32[]{:S(2)}, u32[]{:S(2)}) %collective-permute-start.3) | collective-permute-done | bytes 229408 | tf_op jit(solution)/shard_map/ppermute | solution.py:36
  152.5 2.0 %collective-permute-start.6 = (bf16[4,8,1792]{2,1,0:T(8,128)(2,1)S(1)}, bf16[4,8,1792]{2,1,0:T(8,128)(2,1)S(1)}, u32[]{:S(2)}, u32[]{:S(2)}) collective-permute-start(bf16[4,8,1792]{2,1,0:T(8,128)(2,1)S(1)} %dynamic-slice_bitcast_fusion.3), channel_id=1, source_target_pairs={{0,32},{12,44},{16,48},{28,60},{32,64},{44,76},{48,80},{60,92},{64... | collective-permute-start | bytes 344072 | tf_op jit(solution)/shard_map/ppermute | solution.py:36
  154.6 10.5 %collective-permute-done.6 = bf16[4,8,1792]{2,1,0:T(8,128)(2,1)S(1)} collective-permute-done((bf16[4,8,1792]{2,1,0:T(8,128)(2,1)S(1)}, bf16[4,8,1792]{2,1,0:T(8,128)(2,1)S(1)}, u32[]{:S(2)}, u32[]{:S(2)}) %collective-permute-start.6) | collective-permute-done | bytes 114720 | tf_op jit(solution)/shard_map/ppermute | solution.py:36
  165.8 3.4 %all-to-all-start.3 = ((bf16[4,8,1792]{2,1,0:T(8,128)(2,1)}), bf16[4,8,1792]{2,1,0:T(8,128)(2,1)S(1)}, u32[]{:S(2)}, u32[]{:S(2)}) async-start(bf16[4,8,1792]{2,1,0:T(8,128)(2,1)} %fusion.9), calls=%async_computation.3 | async-start | bytes 229376 | tf_op jit(solution)/shard_map/all_to_all | solution.py:265
  169.9 0.7 divide_convert_fusion
  170.6 23.5 %all-to-all-done.3 = bf16[4,8,1792]{2,1,0:T(8,128)(2,1)S(1)} async-done(((bf16[4,8,1792]{2,1,0:T(8,128)(2,1)}), bf16[4,8,1792]{2,1,0:T(8,128)(2,1)S(1)}, u32[]{:S(2)}, u32[]{:S(2)}) %all-to-all-start.3) | async-done | bytes 114720 | tf_op jit(solution)/shard_map/all_to_all | solution.py:265
  (55 shorter events, 5.6 us)
Async XLA Ops:
  0.6 105.0 %copy-start = (bf16[2,256,512]{2,1,0:T(8,128)(2,1)S(1)}, bf16[2,256,512]{2,1,0:T(8,128)(2,1)}, u32[]{:S(2)}) copy-start(bf16[2,256,512]{2,1,0:T(8,128)(2,1)} %param.12) | copy-start | bytes 1572868
  0.6 97.5 %collective-permute-start = (bf16[288,1792]{1,0:T(8,128)(2,1)}, bf16[288,1792]{1,0:T(8,128)(2,1)S(1)}, u32[]{:S(2)}, u32[]{:S(2)}) collective-permute-start(bf16[288,1792]{1,0:T(8,128)(2,1)} %bitcast.77), channel_id=1, source_target_pairs={{0,4},{4,0},{1,5},{5,1},{2,6},{6,2},{3,7},{7,3},{8,12},{12,8},{9,1... | collective-permute-start | bytes 3096584 | tf_op jit(solution)/shard_map/ppermute | solution.py:46
  2.7 95.4 %collective-permute-start.1 = (bf16[288,1792]{1,0:T(8,128)(2,1)}, bf16[288,1792]{1,0:T(8,128)(2,1)S(1)}, u32[]{:S(2)}, u32[]{:S(2)}) collective-permute-start(bf16[288,1792]{1,0:T(8,128)(2,1)} %bitcast.79), channel_id=1, source_target_pairs={{0,4},{4,0},{1,5},{5,1},{2,6},{6,2},{3,7},{7,3},{8,12},{12,8},{9,1... | collective-permute-start | bytes 3096584 | tf_op jit(solution)/shard_map/ppermute | solution.py:46
  5.3 100.0 %copy-start.7 = (bf16[2,64,256]{2,1,0:T(8,128)(2,1)S(1)}, bf16[2,64,256]{2,1,0:T(8,128)(2,1)}, u32[]{:S(2)}) copy-start(bf16[2,64,256]{2,1,0:T(8,128)(2,1)} %param.13) | copy-start | bytes 196612
  5.3 100.0 %copy-start.8 = (bf16[2,64,128]{2,1,0:T(8,128)(2,1)S(1)}, bf16[2,64,128]{2,1,0:T(8,128)(2,1)}, u32[]{:S(2)}) copy-start(bf16[2,64,128]{2,1,0:T(8,128)(2,1)} %param.11) | copy-start | bytes 98308
  5.3 100.2 %copy-start.9 = (s32[2]{0:T(128)S(1)}, s32[2]{0:T(128)}, u32[]{:S(2)}) copy-start(s32[2]{0:T(128)} %param.14) | copy-start | bytes 28
  5.3 100.3 %copy-start.5 = (bf16[2,128,512]{2,1,0:T(8,128)(2,1)S(1)}, bf16[2,128,512]{2,1,0:T(8,128)(2,1)}, u32[]{:S(2)}) copy-start(bf16[2,128,512]{2,1,0:T(8,128)(2,1)} %param.10) | copy-start | bytes 786436
  98.1 1.2 copy-start.1
  99.3 1.2 copy-start.2
  100.6 0.7 copy-start.3
  106.2 15.5 %all-to-all-start.1 = ((bf16[4,296,256]{2,1,0:T(8,128)(2,1)}), bf16[4,296,256]{2,1,0:T(8,128)(2,1)S(1)}, u32[]{:S(2)}, u32[]{:S(2)}) async-start(bf16[4,296,256]{2,1,0:T(8,128)(2,1)} %projected.1), calls=%async_computation.1 | async-start | bytes 1212416 | tf_op jit(solution)/shard_map/all_to_all | solution.py:50
  110.8 22.1 %collective-permute-start.2 = (bf16[288,1792]{1,0:T(8,128)(2,1)}, bf16[288,1792]{1,0:T(8,128)(2,1)S(1)}, u32[]{:S(2)}, u32[]{:S(2)}) collective-permute-start(bf16[288,1792]{1,0:T(8,128)(2,1)} %param.19), channel_id=1, source_target_pairs={{0,4},{4,0},{1,5},{5,1},{2,6},{6,2},{3,7},{7,3},{8,12},{12,8},{9,1... | collective-permute-start | bytes 3096584 | tf_op jit(solution)/shard_map/ppermute | solution.py:46
  122.6 10.3 %all-to-all-start.2 = ((bf16[4,2,72,256]{3,2,1,0:T(8,128)(2,1)}), bf16[4,2,72,256]{3,2,1,0:T(8,128)(2,1)S(1)}, u32[]{:S(2)}, u32[]{:S(2)}) async-start(bf16[4,2,72,256]{3,2,1,0:T(8,128)(2,1)} %broadcast_in_dim.31), calls=%async_computation.2 | async-start | bytes 589824 | tf_op jit(solution)/shard_map/all_to_all | solution.py:50
  126.2 7.5 %copy-start.4 = (bf16[288,1792]{1,0:T(8,128)(2,1)S(1)}, bf16[288,1792]{1,0:T(8,128)(2,1)}, u32[]{:S(2)}) copy-start(bf16[288,1792]{1,0:T(8,128)(2,1)} %param.19) | copy-start | bytes 3096580
  134.4 12.3 %collective-permute-start.5 = (bf16[8,8,1792]{2,1,0:T(8,128)(2,1)S(1)}, bf16[8,8,1792]{2,1,0:T(8,128)(2,1)S(1)}, u32[]{:S(2)}, u32[]{:S(2)}) collective-permute-start(bf16[8,8,1792]{2,1,0:T(8,128)(2,1)S(1)} %get-tuple-element.21), channel_id=1, source_target_pairs={{0,252},{12,0},{16,12},{28,16},{32,28},{44,32},{48,44},{60,48},{64... | collective-permute-start | bytes 688136 | tf_op jit(solution)/shard_map/ppermute | solution.py:36
  136.4 10.8 %collective-permute-start.4 = (bf16[8,8,1792]{2,1,0:T(8,128)(2,1)S(1)}, bf16[8,8,1792]{2,1,0:T(8,128)(2,1)S(1)}, u32[]{:S(2)}, u32[]{:S(2)}) collective-permute-start(bf16[8,8,1792]{2,1,0:T(8,128)(2,1)S(1)} %get-tuple-element.22), channel_id=1, source_target_pairs={{0,12},{12,16},{16,28},{28,32},{32,44},{44,48},{48,60},{60,64},{64... | collective-permute-start | bytes 688136 | tf_op jit(solution)/shard_map/ppermute | solution.py:36
  140.0 12.4 %collective-permute-start.3 = (bf16[8,8,1792]{2,1,0:T(8,128)(2,1)S(1)}, bf16[8,8,1792]{2,1,0:T(8,128)(2,1)S(1)}, u32[]{:S(2)}, u32[]{:S(2)}) collective-permute-start(bf16[8,8,1792]{2,1,0:T(8,128)(2,1)S(1)} %get-tuple-element.20), channel_id=1, source_target_pairs={{0,16},{12,28},{16,32},{28,44},{32,48},{44,60},{48,64},{60,76},{64... | collective-permute-start | bytes 688136 | tf_op jit(solution)/shard_map/ppermute | solution.py:36
  143.2 11.3 %all-to-all-start = ((bf16[4,2,32,640]{3,2,1,0:T(8,128)(2,1)}), bf16[4,2,32,640]{3,2,1,0:T(8,128)(2,1)S(1)}, u32[]{:S(2)}, u32[]{:S(2)}) async-start(bf16[4,2,32,640]{3,2,1,0:T(8,128)(2,1)} %bitcast.76), calls=%async_computation | async-start | bytes 655360 | tf_op jit(solution)/shard_map/all_to_all | solution.py:50
  152.5 12.6 %collective-permute-start.6 = (bf16[4,8,1792]{2,1,0:T(8,128)(2,1)S(1)}, bf16[4,8,1792]{2,1,0:T(8,128)(2,1)S(1)}, u32[]{:S(2)}, u32[]{:S(2)}) collective-permute-start(bf16[4,8,1792]{2,1,0:T(8,128)(2,1)S(1)} %dynamic-slice_bitcast_fusion.3), channel_id=1, source_target_pairs={{0,32},{12,44},{16,48},{28,60},{32,64},{44,76},{48,80},{60,92},{64... | collective-permute-start | bytes 344072 | tf_op jit(solution)/shard_map/ppermute | solution.py:36
  154.5 39.6 %copy-start.6 = (bf16[8,1792]{1,0:T(8,128)(2,1)S(1)}, bf16[8,1792]{1,0:T(8,128)(2,1)}, u32[]{:S(2)}) copy-start(bf16[8,1792]{1,0:T(8,128)(2,1)} %param.15) | copy-start | bytes 86020
  165.8 28.3 %all-to-all-start.3 = ((bf16[4,8,1792]{2,1,0:T(8,128)(2,1)}), bf16[4,8,1792]{2,1,0:T(8,128)(2,1)S(1)}, u32[]{:S(2)}, u32[]{:S(2)}) async-start(bf16[4,8,1792]{2,1,0:T(8,128)(2,1)} %fusion.9), calls=%async_computation.3 | async-start | bytes 229376 | tf_op jit(solution)/shard_map/all_to_all | solution.py:265

commit v4 on v3

--- a/solution.py
+++ b/solution.py
@@ -146,16 +146,48 @@
     return total.astype(jnp.bfloat16)
 
 
+def stage_kernel(gate_ref, up_ref, gain_ref, both_ref, gain_out_ref, arrived):
+    units = gate_ref.shape[0]
+    copies = [
+        pltpu.make_async_copy(gate_ref, both_ref.at[pl.ds(0, units)], arrived.at[0]),
+        pltpu.make_async_copy(up_ref, both_ref.at[pl.ds(units, units)], arrived.at[1]),
+        pltpu.make_async_copy(gain_ref, gain_out_ref, arrived.at[2]),
+    ]
+    for copy in copies:
+        copy.start()
+    for copy in copies:
+        copy.wait()
+
+
+def staged(gate, up, gain):
+    units, width = gate.shape
+    anywhere = pl.BlockSpec(memory_space=pl.ANY)
+    return pl.pallas_call(
+        stage_kernel,
+        out_shape=(
+            jax.ShapeDtypeStruct((2 * units, width), gate.dtype),
+            jax.ShapeDtypeStruct(gain.shape, gain.dtype),
+        ),
+        in_specs=[anywhere] * 3,
+        out_specs=(anywhere, anywhere),
+        scratch_shapes=[pltpu.SemaphoreType.DMA((3,))],
+        compiler_params=pltpu.CompilerParams(vmem_limit_bytes=1 << 20),
+        name="staged",
+    )(gate, up, gain)
+
+
 def project_kernel(x_ref, gain_ref, *refs):
     *w_refs, out_ref, w_vmem, arrived = refs
-    units = w_refs[0].shape[0]
+    rows = w_refs[0].shape[0]
     copies = [
-        pltpu.make_async_copy(w_ref, w_vmem.at[pl.ds(k * units, units)], arrived.at[k])
+        pltpu.make_async_copy(w_ref, w_vmem.at[pl.ds(k * rows, rows)], arrived.at[k])
         for k, w_ref in enumerate(w_refs)
     ]
     for copy in copies:
         copy.start()
     cols, _, tokens = out_ref.shape
+    projections = 2 * len(copies)
+    units = rows // 2
     share = units // cols
     x = x_ref[...].astype(jnp.float32)
     scaled = (x * gain_ref[...].astype(jnp.float32)).astype(jnp.bfloat16)
@@ -165,13 +197,13 @@
     row = lax.broadcasted_iota(jnp.int32, squares.shape, 0)
     norms = jnp.where(row == 0, coarse, squares - coarse).astype(jnp.bfloat16)
     for c in range(cols):
-        out_ref[c, len(copies) * share :, :] = norms
+        out_ref[c, projections * share :, :] = norms
     for copy in copies:
         copy.wait()
     product = lax.dot_general(
         w_vmem[...], scaled, (((1,), (1,)), ((), ())), preferred_element_type=jnp.float32
     ).astype(jnp.bfloat16)
-    for k in range(len(copies)):
+    for k in range(projections):
         for c in range(cols):
             start = k * units + c * share
             out_ref[c, k * share : (k + 1) * share, :] = product[start : start + share, :]
@@ -179,22 +211,21 @@
 
 def projected(gathered, gain, weights, cols):
     tokens, width = gathered.shape
-    units = weights[0].shape[0]
-    rows = len(weights) * units // cols + 8
+    units = len(weights) * weights[0].shape[0]
     whole = pl.BlockSpec(memory_space=pltpu.VMEM)
     return pl.pallas_call(
         project_kernel,
-        out_shape=jax.ShapeDtypeStruct((cols, rows, tokens), jnp.bfloat16),
-        in_specs=[whole, whole] + [pl.BlockSpec(memory_space=pltpu.HBM)] * len(weights),
+        out_shape=jax.ShapeDtypeStruct((cols, units // cols + 8, tokens), jnp.bfloat16),
+        in_specs=[whole, whole] + [pl.BlockSpec(memory_space=pl.ANY)] * len(weights),
         out_specs=whole,
         scratch_shapes=[
-            pltpu.VMEM((len(weights) * units, width), jnp.bfloat16),
+            pltpu.VMEM((units, width), jnp.bfloat16),
             pltpu.SemaphoreType.DMA((len(weights),)),
         ],
         compiler_params=pltpu.CompilerParams(vmem_limit_bytes=24 << 20),
         cost_estimate=pl.CostEstimate(
-            flops=2 * len(weights) * units * width * tokens,
-            bytes_accessed=2 * len(weights) * units * width,
+            flops=2 * units * width * tokens,
+            bytes_accessed=2 * units * width,
             transcendentals=0,
         ),
         name="projected",
@@ -206,11 +237,11 @@
     rows, width = ffn_rows.shape
     units = w_gate.shape[1]
     share = units // cols
-    into = [w_gate.T, w_up.T]
-    into += [swapped(w) for w in into]
+    into, gain = staged(w_gate.T, w_up.T, norm_gain)
+    into = [into, swapped(into)]
     gathered = gathered_on_lane(ffn_rows)
 
-    packed = projected(gathered, norm_gain, into, cols)
+    packed = projected(gathered, gain, into, cols)
     packed, w_down, *queries = lax.optimization_barrier((packed, w_down, *queries))
     out_of = [w_down, swapped(w_down)]
     total = exchanged(packed)

time: 195 us -> 196 us (level)
  the two profiles are of different devices: /device:TPU:40 before, /device:TPU:161 now
where the time goes in v4:
time: 196 us; the launch traced here: 195 us
  blocking collectives  88.6 us (45%)
  waiting for transfers between devices  51.1 us (26%)
  starting transfers between devices  38.7 us (20%)
  Pallas kernels  5.14 us (3%)
  local copies, waits for them, and re-layouts  4.93 us (3%)
  other arithmetic  3.37 us (2%)
  matrix products  2.22 us (1%)
    all_gather x1, blocking collectives, gathered_on_lane(): return lax.all_gather(x, ROW, axis_index_groups=lanes, axis=0, tiled=True)  88.6 us
    all_to_all x1, waiting for transfers between devices, on_device(): pieces = lax.all_to_all(row_major(near), FAR, 0, 0, tiled=True)  26.3 us
    ppermute x4, starting transfers between devices, along_lane(): return lax.ppermute(x, ROW, pairs)  15.5 us
    all_to_all x3, waiting for transfers between devices, exchanged(): return lax.all_to_all(pieces, COL, split_axis=0, concat_axis=0, tiled=True)  12.8 us
    ppermute x4, waiting for transfers between devices, along_lane(): return lax.ppermute(x, ROW, pairs)  12 us
    all_to_all x3, starting transfers between devices, exchanged(): return lax.all_to_all(pieces, COL, split_axis=0, concat_axis=0, tiled=True)  11.4 us
    all_to_all x1, starting transfers between devices, on_device(): pieces = lax.all_to_all(row_major(near), FAR, 0, 0, tiled=True)  6.82 us
    ppermute x2, starting transfers between devices, swapped(): return lax.ppermute(x, CORE, [(0, 1), (1, 0)])  4.98 us
  transfers between devices with their start and end apart: 10, of which 5 were waited for; matrix products, arithmetic and copies ran while one was open for 2% of the time, Pallas kernels for 0%

profile of v4, /device:TPU:161, one launch (start us, length us, event | category | flops | bytes accessed | tf_op | source)
XLA Modules:
  0.0 195.1 jit_solution(14878811367955124494)
XLA Ops:
  0.7 1.3 copy-done.1
  1.9 1.2 copy-done.2
  3.1 0.7 copy-done.3
  3.8 0.8 staged.1
  4.6 2.5 %collective-permute-start = (bf16[576,1792]{1,0:T(8,128)(2,1)S(1)}, bf16[576,1792]{1,0:T(8,128)(2,1)}, u32[]{:S(2)}, u32[]{:S(2)}) collective-permute-start(bf16[576,1792]{1,0:T(8,128)(2,1)S(1)} %get-tuple-element.12.refs_0_), channel_id=1, source_target_pairs={{0,4},{4,0},{1,5},{5,1},{2,6},{6,2},{3,7},{7,3},{8,12},{12,8},{9,1... | collective-permute-start | bytes 6193160 | tf_op jit(solution)/shard_map/ppermute | solution.py:46
  7.3 88.6 %all_gather.3.x_ref = bf16[256,1792]{1,0:T(8,128)(2,1)S(1)} all-gather(bf16[8,1792]{1,0:T(8,128)(2,1)S(1)} %copy-done.6), channel_id=1, replica_groups={{0,12,16,28,32,44,48,60,64,76,80,92,96,108,112,124,128,140,144,156,160,..., dimensions={0}, use_global_device_ids=true | all-gather | bytes 946176 | tf_op jit(solution)/shard_map/all_gather | solution.py:42
  95.9 4.4 %projected.1 = bf16[4,296,256]{2,1,0:T(8,128)(2,1)} custom-call(bf16[256,1792]{1,0:T(8,128)(2,1)S(1)} %all_gather.3.x_ref, bf16[1792]{0:T(1024)(128)(2,1)S(1)} %get-tuple-element.11.gain_ref, bf16[576,1792]{1,0:T(8,128)(2,1)S(1)} %get-tuple-element.12.refs_0_, bf16[576,1792]{1,0:T(8,128)(2,1)} %collective-permute-done.refs_1_), custom_call_target="tpu_custom_call" | custom-call | flops 1056964608 | bytes 4128768 | tf_op jit(solution)/shard_map/projected/pallas_call | solution.py:216
  101.3 4.3 %all-to-all-start.1 = ((bf16[4,296,256]{2,1,0:T(8,128)(2,1)}), bf16[4,296,256]{2,1,0:T(8,128)(2,1)S(1)}, u32[]{:S(2)}, u32[]{:S(2)}) async-start(bf16[4,296,256]{2,1,0:T(8,128)(2,1)} %projected.1), calls=%async_computation.1 | async-start | bytes 1212416 | tf_op jit(solution)/shard_map/all_to_all | solution.py:50
  105.6 2.4 %collective-permute-start.1 = (bf16[288,1792]{1,0:T(8,128)(2,1)}, bf16[288,1792]{1,0:T(8,128)(2,1)S(1)}, u32[]{:S(2)}, u32[]{:S(2)}) collective-permute-start(bf16[288,1792]{1,0:T(8,128)(2,1)} %param.19), channel_id=1, source_target_pairs={{0,4},{4,0},{1,5},{5,1},{2,6},{6,2},{3,7},{7,3},{8,12},{12,8},{9,1... | collective-permute-start | bytes 3096584 | tf_op jit(solution)/shard_map/ppermute | solution.py:46
  108.3 7.2 %all-to-all-done.1 = bf16[4,296,256]{2,1,0:T(8,128)(2,1)S(1)} async-done(((bf16[4,296,256]{2,1,0:T(8,128)(2,1)}), bf16[4,296,256]{2,1,0:T(8,128)(2,1)S(1)}, u32[]{:S(2)}, u32[]{:S(2)}) %all-to-all-start.1) | async-done | bytes 606240 | tf_op jit(solution)/shard_map/all_to_all | solution.py:50
  115.7 0.7 broadcast_in_dim.31
  116.4 3.5 %all-to-all-start.2 = ((bf16[4,2,72,256]{3,2,1,0:T(8,128)(2,1)}), bf16[4,2,72,256]{3,2,1,0:T(8,128)(2,1)S(1)}, u32[]{:S(2)}, u32[]{:S(2)}) async-start(bf16[4,2,72,256]{3,2,1,0:T(8,128)(2,1)} %broadcast_in_dim.31), calls=%async_computation.2 | async-start | bytes 589824 | tf_op jit(solution)/shard_map/all_to_all | solution.py:50
  120.0 5.6 %all-to-all-done.2 = bf16[4,2,72,256]{3,2,1,0:T(8,128)(2,1)S(1)} async-done(((bf16[4,2,72,256]{3,2,1,0:T(8,128)(2,1)}), bf16[4,2,72,256]{3,2,1,0:T(8,128)(2,1)S(1)}, u32[]{:S(2)}, u32[]{:S(2)}) %all-to-all-start.2) | async-done | bytes 294944 | tf_op jit(solution)/shard_map/all_to_all | solution.py:50
  127.0 7.1 %collective-permute-start.4 = (bf16[8,8,1792]{2,1,0:T(8,128)(2,1)S(1)}, bf16[8,8,1792]{2,1,0:T(8,128)(2,1)S(1)}, u32[]{:S(2)}, u32[]{:S(2)}) collective-permute-start(bf16[8,8,1792]{2,1,0:T(8,128)(2,1)S(1)} %get-tuple-element.25), channel_id=1, source_target_pairs={{0,252},{12,0},{16,12},{28,16},{32,28},{44,32},{48,44},{60,48},{64... | collective-permute-start | bytes 688136 | tf_op jit(solution)/shard_map/ppermute | solution.py:36
  134.2 2.0 %collective-permute-start.3 = (bf16[8,8,1792]{2,1,0:T(8,128)(2,1)S(1)}, bf16[8,8,1792]{2,1,0:T(8,128)(2,1)S(1)}, u32[]{:S(2)}, u32[]{:S(2)}) collective-permute-start(bf16[8,8,1792]{2,1,0:T(8,128)(2,1)S(1)} %get-tuple-element.26), channel_id=1, source_target_pairs={{0,12},{12,16},{16,28},{28,32},{32,44},{44,48},{48,60},{60,64},{64... | collective-permute-start | bytes 688136 | tf_op jit(solution)/shard_map/ppermute | solution.py:36
  136.1 2.2 %collective-permute-start.2 = (bf16[8,8,1792]{2,1,0:T(8,128)(2,1)S(1)}, bf16[8,8,1792]{2,1,0:T(8,128)(2,1)S(1)}, u32[]{:S(2)}, u32[]{:S(2)}) collective-permute-start(bf16[8,8,1792]{2,1,0:T(8,128)(2,1)S(1)} %get-tuple-element.24), channel_id=1, source_target_pairs={{0,16},{12,28},{16,32},{28,44},{32,48},{44,60},{48,64},{60,76},{64... | collective-permute-start | bytes 688136 | tf_op jit(solution)/shard_map/ppermute | solution.py:36
  138.5 0.7 copy.40
  139.2 3.5 %all-to-all-start = ((bf16[4,2,32,640]{3,2,1,0:T(8,128)(2,1)}), bf16[4,2,32,640]{3,2,1,0:T(8,128)(2,1)S(1)}, u32[]{:S(2)}, u32[]{:S(2)}) async-start(bf16[4,2,32,640]{3,2,1,0:T(8,128)(2,1)} %bitcast.76), calls=%async_computation | async-start | bytes 655360 | tf_op jit(solution)/shard_map/all_to_all | solution.py:50
  142.8 5.3 %collective-permute-done.2 = bf16[8,8,1792]{2,1,0:T(8,128)(2,1)S(1)} collective-permute-done((bf16[8,8,1792]{2,1,0:T(8,128)(2,1)S(1)}, bf16[8,8,1792]{2,1,0:T(8,128)(2,1)S(1)}, u32[]{:S(2)}, u32[]{:S(2)}) %collective-permute-start.2) | collective-permute-done | bytes 229408 | tf_op jit(solution)/shard_map/ppermute | solution.py:36
  148.2 4.3 %collective-permute-start.5 = (bf16[4,8,1792]{2,1,0:T(8,128)(2,1)S(1)}, bf16[4,8,1792]{2,1,0:T(8,128)(2,1)S(1)}, u32[]{:S(2)}, u32[]{:S(2)}) collective-permute-start(bf16[4,8,1792]{2,1,0:T(8,128)(2,1)S(1)} %dynamic-slice_bitcast_fusion.3), channel_id=1, source_target_pairs={{0,32},{12,44},{16,48},{28,60},{32,64},{44,76},{48,80},{60,92},{64... | collective-permute-start | bytes 344072 | tf_op jit(solution)/shard_map/ppermute | solution.py:36
  152.6 6.7 %collective-permute-done.5 = bf16[4,8,1792]{2,1,0:T(8,128)(2,1)S(1)} collective-permute-done((bf16[4,8,1792]{2,1,0:T(8,128)(2,1)S(1)}, bf16[4,8,1792]{2,1,0:T(8,128)(2,1)S(1)}, u32[]{:S(2)}, u32[]{:S(2)}) %collective-permute-start.5) | collective-permute-done | bytes 114720 | tf_op jit(solution)/shard_map/ppermute | solution.py:36
  159.9 6.8 %all-to-all-start.3 = ((bf16[4,8,1792]{2,1,0:T(8,128)(2,1)}), bf16[4,8,1792]{2,1,0:T(8,128)(2,1)S(1)}, u32[]{:S(2)}, u32[]{:S(2)}) async-start(bf16[4,8,1792]{2,1,0:T(8,128)(2,1)} %fusion.9), calls=%async_computation.3 | async-start | bytes 229376 | tf_op jit(solution)/shard_map/all_to_all | solution.py:296
  167.4 0.7 divide_convert_fusion
  168.1 26.3 %all-to-all-done.3 = bf16[4,8,1792]{2,1,0:T(8,128)(2,1)S(1)} async-done(((bf16[4,8,1792]{2,1,0:T(8,128)(2,1)}), bf16[4,8,1792]{2,1,0:T(8,128)(2,1)S(1)}, u32[]{:S(2)}, u32[]{:S(2)}) %all-to-all-start.3) | async-done | bytes 114720 | tf_op jit(solution)/shard_map/all_to_all | solution.py:296
  (54 shorter events, 5.2 us)
Async XLA Ops:
  0.6 100.0 %copy-start = (bf16[2,256,512]{2,1,0:T(8,128)(2,1)S(1)}, bf16[2,256,512]{2,1,0:T(8,128)(2,1)}, u32[]{:S(2)}) copy-start(bf16[2,256,512]{2,1,0:T(8,128)(2,1)} %param.12) | copy-start | bytes 1572868
  0.6 1.3 copy-start.1
  1.9 1.2 copy-start.2
  3.1 0.7 copy-start.3
  3.8 3.4 %copy-start.6 = (bf16[8,1792]{1,0:T(8,128)(2,1)S(1)}, bf16[8,1792]{1,0:T(8,128)(2,1)}, u32[]{:S(2)}) copy-start(bf16[8,1792]{1,0:T(8,128)(2,1)} %param.15) | copy-start | bytes 86020
  4.6 91.3 %collective-permute-start = (bf16[576,1792]{1,0:T(8,128)(2,1)S(1)}, bf16[576,1792]{1,0:T(8,128)(2,1)}, u32[]{:S(2)}, u32[]{:S(2)}) collective-permute-start(bf16[576,1792]{1,0:T(8,128)(2,1)S(1)} %get-tuple-element.12.refs_0_), channel_id=1, source_target_pairs={{0,4},{4,0},{1,5},{5,1},{2,6},{6,2},{3,7},{7,3},{8,12},{12,8},{9,1... | collective-permute-start | bytes 6193160 | tf_op jit(solution)/shard_map/ppermute | solution.py:46
  95.9 4.4 %copy-start.7 = (bf16[2,64,256]{2,1,0:T(8,128)(2,1)S(1)}, bf16[2,64,256]{2,1,0:T(8,128)(2,1)}, u32[]{:S(2)}) copy-start(bf16[2,64,256]{2,1,0:T(8,128)(2,1)} %param.13) | copy-start | bytes 196612
  95.9 4.4 %copy-start.8 = (bf16[2,64,128]{2,1,0:T(8,128)(2,1)S(1)}, bf16[2,64,128]{2,1,0:T(8,128)(2,1)}, u32[]{:S(2)}) copy-start(bf16[2,64,128]{2,1,0:T(8,128)(2,1)} %param.11) | copy-start | bytes 98308
  95.9 4.7 %copy-start.9 = (s32[2]{0:T(128)S(1)}, s32[2]{0:T(128)}, u32[]{:S(2)}) copy-start(s32[2]{0:T(128)} %param.14) | copy-start | bytes 28
  95.9 4.8 %copy-start.5 = (bf16[2,128,512]{2,1,0:T(8,128)(2,1)S(1)}, bf16[2,128,512]{2,1,0:T(8,128)(2,1)}, u32[]{:S(2)}) copy-start(bf16[2,128,512]{2,1,0:T(8,128)(2,1)} %param.10) | copy-start | bytes 786436
  101.3 14.3 %all-to-all-start.1 = ((bf16[4,296,256]{2,1,0:T(8,128)(2,1)}), bf16[4,296,256]{2,1,0:T(8,128)(2,1)S(1)}, u32[]{:S(2)}, u32[]{:S(2)}) async-start(bf16[4,296,256]{2,1,0:T(8,128)(2,1)} %projected.1), calls=%async_computation.1 | async-start | bytes 1212416 | tf_op jit(solution)/shard_map/all_to_all | solution.py:50
  105.6 20.0 %collective-permute-start.1 = (bf16[288,1792]{1,0:T(8,128)(2,1)}, bf16[288,1792]{1,0:T(8,128)(2,1)S(1)}, u32[]{:S(2)}, u32[]{:S(2)}) collective-permute-start(bf16[288,1792]{1,0:T(8,128)(2,1)} %param.19), channel_id=1, source_target_pairs={{0,4},{4,0},{1,5},{5,1},{2,6},{6,2},{3,7},{7,3},{8,12},{12,8},{9,1... | collective-permute-start | bytes 3096584 | tf_op jit(solution)/shard_map/ppermute | solution.py:46
  116.4 9.2 %all-to-all-start.2 = ((bf16[4,2,72,256]{3,2,1,0:T(8,128)(2,1)}), bf16[4,2,72,256]{3,2,1,0:T(8,128)(2,1)S(1)}, u32[]{:S(2)}, u32[]{:S(2)}) async-start(bf16[4,2,72,256]{3,2,1,0:T(8,128)(2,1)} %broadcast_in_dim.31), calls=%async_computation.2 | async-start | bytes 589824 | tf_op jit(solution)/shard_map/all_to_all | solution.py:50
  120.0 6.3 %copy-start.4 = (bf16[288,1792]{1,0:T(8,128)(2,1)S(1)}, bf16[288,1792]{1,0:T(8,128)(2,1)}, u32[]{:S(2)}) copy-start(bf16[288,1792]{1,0:T(8,128)(2,1)} %param.19) | copy-start | bytes 3096580
  127.0 15.7 %collective-permute-start.4 = (bf16[8,8,1792]{2,1,0:T(8,128)(2,1)S(1)}, bf16[8,8,1792]{2,1,0:T(8,128)(2,1)S(1)}, u32[]{:S(2)}, u32[]{:S(2)}) collective-permute-start(bf16[8,8,1792]{2,1,0:T(8,128)(2,1)S(1)} %get-tuple-element.25), channel_id=1, source_target_pairs={{0,252},{12,0},{16,12},{28,16},{32,28},{44,32},{48,44},{60,48},{64... | collective-permute-start | bytes 688136 | tf_op jit(solution)/shard_map/ppermute | solution.py:36
  134.2 8.6 %collective-permute-start.3 = (bf16[8,8,1792]{2,1,0:T(8,128)(2,1)S(1)}, bf16[8,8,1792]{2,1,0:T(8,128)(2,1)S(1)}, u32[]{:S(2)}, u32[]{:S(2)}) collective-permute-start(bf16[8,8,1792]{2,1,0:T(8,128)(2,1)S(1)} %get-tuple-element.26), channel_id=1, source_target_pairs={{0,12},{12,16},{16,28},{28,32},{32,44},{44,48},{48,60},{60,64},{64... | collective-permute-start | bytes 688136 | tf_op jit(solution)/shard_map/ppermute | solution.py:36
  136.1 12.0 %collective-permute-start.2 = (bf16[8,8,1792]{2,1,0:T(8,128)(2,1)S(1)}, bf16[8,8,1792]{2,1,0:T(8,128)(2,1)S(1)}, u32[]{:S(2)}, u32[]{:S(2)}) collective-permute-start(bf16[8,8,1792]{2,1,0:T(8,128)(2,1)S(1)} %get-tuple-element.24), channel_id=1, source_target_pairs={{0,16},{12,28},{16,32},{28,44},{32,48},{44,60},{48,64},{60,76},{64... | collective-permute-start | bytes 688136 | tf_op jit(solution)/shard_map/ppermute | solution.py:36
  139.2 13.3 %all-to-all-start = ((bf16[4,2,32,640]{3,2,1,0:T(8,128)(2,1)}), bf16[4,2,32,640]{3,2,1,0:T(8,128)(2,1)S(1)}, u32[]{:S(2)}, u32[]{:S(2)}) async-start(bf16[4,2,32,640]{3,2,1,0:T(8,128)(2,1)} %bitcast.76), calls=%async_computation | async-start | bytes 655360 | tf_op jit(solution)/shard_map/all_to_all | solution.py:50
  148.2 11.0 %collective-permute-start.5 = (bf16[4,8,1792]{2,1,0:T(8,128)(2,1)S(1)}, bf16[4,8,1792]{2,1,0:T(8,128)(2,1)S(1)}, u32[]{:S(2)}, u32[]{:S(2)}) collective-permute-start(bf16[4,8,1792]{2,1,0:T(8,128)(2,1)S(1)} %dynamic-slice_bitcast_fusion.3), channel_id=1, source_target_pairs={{0,32},{12,44},{16,48},{28,60},{32,64},{44,76},{48,80},{60,92},{64... | collective-permute-start | bytes 344072 | tf_op jit(solution)/shard_map/ppermute | solution.py:36
  159.9 34.5 %all-to-all-start.3 = ((bf16[4,8,1792]{2,1,0:T(8,128)(2,1)}), bf16[4,8,1792]{2,1,0:T(8,128)(2,1)S(1)}, u32[]{:S(2)}, u32[]{:S(2)}) async-start(bf16[4,8,1792]{2,1,0:T(8,128)(2,1)} %fusion.9), calls=%async_computation.3 | async-start | bytes 229376 | tf_op jit(solution)/shard_map/all_to_all | solution.py:296

commit v5 on v4

--- a/solution.py
+++ b/solution.py
@@ -176,18 +176,11 @@
     )(gate, up, gain)
 
 
-def project_kernel(x_ref, gain_ref, *refs):
-    *w_refs, out_ref, w_vmem, arrived = refs
-    rows = w_refs[0].shape[0]
-    copies = [
-        pltpu.make_async_copy(w_ref, w_vmem.at[pl.ds(k * rows, rows)], arrived.at[k])
-        for k, w_ref in enumerate(w_refs)
-    ]
-    for copy in copies:
-        copy.start()
+def project_kernel(x_ref, gain_ref, own_ref, other_ref, out_ref, other_vmem, arrived):
+    copy = pltpu.make_async_copy(other_ref, other_vmem, arrived)
+    copy.start()
     cols, _, tokens = out_ref.shape
-    projections = 2 * len(copies)
-    units = rows // 2
+    units = own_ref.shape[0] // 2
     share = units // cols
     x = x_ref[...].astype(jnp.float32)
     scaled = (x * gain_ref[...].astype(jnp.float32)).astype(jnp.bfloat16)
@@ -197,31 +190,33 @@
     row = lax.broadcasted_iota(jnp.int32, squares.shape, 0)
     norms = jnp.where(row == 0, coarse, squares - coarse).astype(jnp.bfloat16)
     for c in range(cols):
-        out_ref[c, projections * share :, :] = norms
-    for copy in copies:
-        copy.wait()
-    product = lax.dot_general(
-        w_vmem[...], scaled, (((1,), (1,)), ((), ())), preferred_element_type=jnp.float32
-    ).astype(jnp.bfloat16)
-    for k in range(projections):
-        for c in range(cols):
-            start = k * units + c * share
-            out_ref[c, k * share : (k + 1) * share, :] = product[start : start + share, :]
-
-
-def projected(gathered, gain, weights, cols):
+        out_ref[c, 4 * share :, :] = norms
+
+    def write(weights, first):
+        product = lax.dot_general(
+            weights, scaled, (((1,), (1,)), ((), ())), preferred_element_type=jnp.float32
+        ).astype(jnp.bfloat16)
+        for k in range(2):
+            for c in range(cols):
+                start = k * units + c * share
+                to = (first + k) * share
+                out_ref[c, to : to + share, :] = product[start : start + share, :]
+
+    write(own_ref[...], 0)
+    copy.wait()
+    write(other_vmem[...], 2)
+
+
+def projected(gathered, gain, own, other, cols):
     tokens, width = gathered.shape
-    units = len(weights) * weights[0].shape[0]
+    units = own.shape[0] + other.shape[0]
     whole = pl.BlockSpec(memory_space=pltpu.VMEM)
     return pl.pallas_call(
         project_kernel,
         out_shape=jax.ShapeDtypeStruct((cols, units // cols + 8, tokens), jnp.bfloat16),
-        in_specs=[whole, whole] + [pl.BlockSpec(memory_space=pl.ANY)] * len(weights),
+        in_specs=[whole, whole, whole, pl.BlockSpec(memory_space=pl.ANY)],
         out_specs=whole,
-        scratch_shapes=[
-            pltpu.VMEM((units, width), jnp.bfloat16),
-            pltpu.SemaphoreType.DMA((len(weights),)),
-        ],
+        scratch_shapes=[pltpu.VMEM(other.shape, other.dtype), pltpu.SemaphoreType.DMA],
         compiler_params=pltpu.CompilerParams(vmem_limit_bytes=24 << 20),
         cost_estimate=pl.CostEstimate(
             flops=2 * units * width * tokens,
@@ -229,7 +224,7 @@
             transcendentals=0,
         ),
         name="projected",
-    )(gathered, gain, *weights)
+    )(gathered, gain, own, other)
 
 
 def feed_forward(ffn_rows, norm_gain, w_gate, w_up, w_down, queries):
@@ -238,10 +233,10 @@
     units = w_gate.shape[1]
     share = units // cols
     into, gain = staged(w_gate.T, w_up.T, norm_gain)
-    into = [into, swapped(into)]
+    partners = swapped(into)
     gathered = gathered_on_lane(ffn_rows)
 
-    packed = projected(gathered, gain, into, cols)
+    packed = projected(gathered, gain, into, partners, cols)
     packed, w_down, *queries = lax.optimization_barrier((packed, w_down, *queries))
     out_of = [w_down, swapped(w_down)]
     total = exchanged(packed)

time: 196 us -> 195 us (level)
  the two profiles are of different devices: /device:TPU:161 before, /device:TPU:163 now
where the time goes in v5:
time: 195 us; the launch traced here: 194 us
  blocking collectives  88.6 us (45%)
  waiting for transfers between devices  47.6 us (24%)
  starting transfers between devices  41.1 us (21%)
  Pallas kernels  5.54 us (3%)
  local copies, waits for them, and re-layouts  4.93 us (3%)
  other arithmetic  3.37 us (2%)
  matrix products  2.21 us (1%)
    all_gather x1, blocking collectives, gathered_on_lane(): return lax.all_gather(x, ROW, axis_index_groups=lanes, axis=0, tiled=True)  88.6 us
    all_to_all x1, waiting for transfers between devices, on_device(): pieces = lax.all_to_all(row_major(near), FAR, 0, 0, tiled=True)  26.3 us
    ppermute x4, starting transfers between devices, along_lane(): return lax.ppermute(x, ROW, pairs)  15.4 us
    all_to_all x3, starting transfers between devices, exchanged(): return lax.all_to_all(pieces, COL, split_axis=0, concat_axis=0, tiled=True)  13.6 us
    ppermute x4, waiting for transfers between devices, along_lane(): return lax.ppermute(x, ROW, pairs)  10.9 us
    all_to_all x3, waiting for transfers between devices, exchanged(): return lax.all_to_all(pieces, COL, split_axis=0, concat_axis=0, tiled=True)  10.4 us
    all_to_all x1, starting transfers between devices, on_device(): pieces = lax.all_to_all(row_major(near), FAR, 0, 0, tiled=True)  6.82 us
    ppermute x2, starting transfers between devices, swapped(): return lax.ppermute(x, CORE, [(0, 1), (1, 0)])  5.25 us
  transfers between devices with their start and end apart: 10, of which 5 were waited for; matrix products, arithmetic and copies ran while one was open for 2% of the time, Pallas kernels for 0%

profile of v5, /device:TPU:163, one launch (start us, length us, event | category | flops | bytes accessed | tf_op | source)
XLA Modules:
  0.0 194.4 jit_solution(11786420593761307976)
XLA Ops:
  0.7 1.3 copy-done.1
  1.9 1.2 copy-done.2
  3.1 0.7 copy-done.3
  3.8 0.8 staged.1
  4.6 2.5 %collective-permute-start = (bf16[576,1792]{1,0:T(8,128)(2,1)S(1)}, bf16[576,1792]{1,0:T(8,128)(2,1)}, u32[]{:S(2)}, u32[]{:S(2)}) collective-permute-start(bf16[576,1792]{1,0:T(8,128)(2,1)S(1)} %get-tuple-element.12.own_ref), channel_id=1, source_target_pairs={{0,4},{4,0},{1,5},{5,1},{2,6},{6,2},{3,7},{7,3},{8,12},{12,8},{9,1... | collective-permute-start | bytes 6193160 | tf_op jit(solution)/shard_map/ppermute | solution.py:46
  7.3 88.6 %all_gather.3.x_ref = bf16[256,1792]{1,0:T(8,128)(2,1)S(1)} all-gather(bf16[8,1792]{1,0:T(8,128)(2,1)S(1)} %copy-done.6), channel_id=1, replica_groups={{0,12,16,28,32,44,48,60,64,76,80,92,96,108,112,124,128,140,144,156,160,..., dimensions={0}, use_global_device_ids=true | all-gather | bytes 946176 | tf_op jit(solution)/shard_map/all_gather | solution.py:42
  95.9 4.8 %projected.1 = bf16[4,296,256]{2,1,0:T(8,128)(2,1)} custom-call(bf16[256,1792]{1,0:T(8,128)(2,1)S(1)} %all_gather.3.x_ref, bf16[1792]{0:T(1024)(128)(2,1)S(1)} %get-tuple-element.11.gain_ref, bf16[576,1792]{1,0:T(8,128)(2,1)S(1)} %get-tuple-element.12.own_ref, bf16[576,1792]{1,0:T(8,128)(2,1)} %collective-permute-done.other_ref), custom_call_target="tpu_custom_call" | custom-call | flops 1056964608 | bytes 4128768 | tf_op jit(solution)/shard_map/projected/pallas_call | solution.py:214
  101.7 4.4 %all-to-all-start.1 = ((bf16[4,296,256]{2,1,0:T(8,128)(2,1)}), bf16[4,296,256]{2,1,0:T(8,128)(2,1)S(1)}, u32[]{:S(2)}, u32[]{:S(2)}) async-start(bf16[4,296,256]{2,1,0:T(8,128)(2,1)} %projected.1), calls=%async_computation.1 | async-start | bytes 1212416 | tf_op jit(solution)/shard_map/all_to_all | solution.py:50
  106.1 2.7 %collective-permute-start.1 = (bf16[288,1792]{1,0:T(8,128)(2,1)}, bf16[288,1792]{1,0:T(8,128)(2,1)S(1)}, u32[]{:S(2)}, u32[]{:S(2)}) collective-permute-start(bf16[288,1792]{1,0:T(8,128)(2,1)} %param.19), channel_id=1, source_target_pairs={{0,4},{4,0},{1,5},{5,1},{2,6},{6,2},{3,7},{7,3},{8,12},{12,8},{9,1... | collective-permute-start | bytes 3096584 | tf_op jit(solution)/shard_map/ppermute | solution.py:46
  109.1 5.8 %all-to-all-done.1 = bf16[4,296,256]{2,1,0:T(8,128)(2,1)S(1)} async-done(((bf16[4,296,256]{2,1,0:T(8,128)(2,1)}), bf16[4,296,256]{2,1,0:T(8,128)(2,1)S(1)}, u32[]{:S(2)}, u32[]{:S(2)}) %all-to-all-start.1) | async-done | bytes 606240 | tf_op jit(solution)/shard_map/all_to_all | solution.py:50
  115.0 0.7 broadcast_in_dim.31
  115.8 4.6 %all-to-all-start.2 = ((bf16[4,2,72,256]{3,2,1,0:T(8,128)(2,1)}), bf16[4,2,72,256]{3,2,1,0:T(8,128)(2,1)S(1)}, u32[]{:S(2)}, u32[]{:S(2)}) async-start(bf16[4,2,72,256]{3,2,1,0:T(8,128)(2,1)} %broadcast_in_dim.31), calls=%async_computation.2 | async-start | bytes 589824 | tf_op jit(solution)/shard_map/all_to_all | solution.py:50
  120.4 4.6 %all-to-all-done.2 = bf16[4,2,72,256]{3,2,1,0:T(8,128)(2,1)S(1)} async-done(((bf16[4,2,72,256]{3,2,1,0:T(8,128)(2,1)}), bf16[4,2,72,256]{3,2,1,0:T(8,128)(2,1)S(1)}, u32[]{:S(2)}, u32[]{:S(2)}) %all-to-all-start.2) | async-done | bytes 294944 | tf_op jit(solution)/shard_map/all_to_all | solution.py:50
  126.4 7.1 %collective-permute-start.4 = (bf16[8,8,1792]{2,1,0:T(8,128)(2,1)S(1)}, bf16[8,8,1792]{2,1,0:T(8,128)(2,1)S(1)}, u32[]{:S(2)}, u32[]{:S(2)}) collective-permute-start(bf16[8,8,1792]{2,1,0:T(8,128)(2,1)S(1)} %get-tuple-element.25), channel_id=1, source_target_pairs={{0,252},{12,0},{16,12},{28,16},{32,28},{44,32},{48,44},{60,48},{64... | collective-permute-start | bytes 688136 | tf_op jit(solution)/shard_map/ppermute | solution.py:36
  133.5 2.0 %collective-permute-start.3 = (bf16[8,8,1792]{2,1,0:T(8,128)(2,1)S(1)}, bf16[8,8,1792]{2,1,0:T(8,128)(2,1)S(1)}, u32[]{:S(2)}, u32[]{:S(2)}) collective-permute-start(bf16[8,8,1792]{2,1,0:T(8,128)(2,1)S(1)} %get-tuple-element.26), channel_id=1, source_target_pairs={{0,12},{12,16},{16,28},{28,32},{32,44},{44,48},{48,60},{60,64},{64... | collective-permute-start | bytes 688136 | tf_op jit(solution)/shard_map/ppermute | solution.py:36
  135.5 2.1 %collective-permute-start.2 = (bf16[8,8,1792]{2,1,0:T(8,128)(2,1)S(1)}, bf16[8,8,1792]{2,1,0:T(8,128)(2,1)S(1)}, u32[]{:S(2)}, u32[]{:S(2)}) collective-permute-start(bf16[8,8,1792]{2,1,0:T(8,128)(2,1)S(1)} %get-tuple-element.24), channel_id=1, source_target_pairs={{0,16},{12,28},{16,32},{28,44},{32,48},{44,60},{48,64},{60,76},{64... | collective-permute-start | bytes 688136 | tf_op jit(solution)/shard_map/ppermute | solution.py:36
  137.8 0.7 copy.40
  138.6 4.6 %all-to-all-start = ((bf16[4,2,32,640]{3,2,1,0:T(8,128)(2,1)}), bf16[4,2,32,640]{3,2,1,0:T(8,128)(2,1)S(1)}, u32[]{:S(2)}, u32[]{:S(2)}) async-start(bf16[4,2,32,640]{3,2,1,0:T(8,128)(2,1)} %bitcast.76), calls=%async_computation | async-start | bytes 655360 | tf_op jit(solution)/shard_map/all_to_all | solution.py:50
  143.2 4.2 %collective-permute-done.2 = bf16[8,8,1792]{2,1,0:T(8,128)(2,1)S(1)} collective-permute-done((bf16[8,8,1792]{2,1,0:T(8,128)(2,1)S(1)}, bf16[8,8,1792]{2,1,0:T(8,128)(2,1)S(1)}, u32[]{:S(2)}, u32[]{:S(2)}) %collective-permute-start.2) | collective-permute-done | bytes 229408 | tf_op jit(solution)/shard_map/ppermute | solution.py:36
  147.6 4.2 %collective-permute-start.5 = (bf16[4,8,1792]{2,1,0:T(8,128)(2,1)S(1)}, bf16[4,8,1792]{2,1,0:T(8,128)(2,1)S(1)}, u32[]{:S(2)}, u32[]{:S(2)}) collective-permute-start(bf16[4,8,1792]{2,1,0:T(8,128)(2,1)S(1)} %dynamic-slice_bitcast_fusion.3), channel_id=1, source_target_pairs={{0,32},{12,44},{16,48},{28,60},{32,64},{44,76},{48,80},{60,92},{64... | collective-permute-start | bytes 344072 | tf_op jit(solution)/shard_map/ppermute | solution.py:36
  151.9 6.7 %collective-permute-done.5 = bf16[4,8,1792]{2,1,0:T(8,128)(2,1)S(1)} collective-permute-done((bf16[4,8,1792]{2,1,0:T(8,128)(2,1)S(1)}, bf16[4,8,1792]{2,1,0:T(8,128)(2,1)S(1)}, u32[]{:S(2)}, u32[]{:S(2)}) %collective-permute-start.5) | collective-permute-done | bytes 114720 | tf_op jit(solution)/shard_map/ppermute | solution.py:36
  159.2 6.8 %all-to-all-start.3 = ((bf16[4,8,1792]{2,1,0:T(8,128)(2,1)}), bf16[4,8,1792]{2,1,0:T(8,128)(2,1)S(1)}, u32[]{:S(2)}, u32[]{:S(2)}) async-start(bf16[4,8,1792]{2,1,0:T(8,128)(2,1)} %fusion.9), calls=%async_computation.3 | async-start | bytes 229376 | tf_op jit(solution)/shard_map/all_to_all | solution.py:291
  166.7 0.7 divide_convert_fusion
  167.4 26.3 %all-to-all-done.3 = bf16[4,8,1792]{2,1,0:T(8,128)(2,1)S(1)} async-done(((bf16[4,8,1792]{2,1,0:T(8,128)(2,1)}), bf16[4,8,1792]{2,1,0:T(8,128)(2,1)S(1)}, u32[]{:S(2)}, u32[]{:S(2)}) %all-to-all-start.3) | async-done | bytes 114720 | tf_op jit(solution)/shard_map/all_to_all | solution.py:291
  (54 shorter events, 5.2 us)
Async XLA Ops:
  0.6 100.4 %copy-start = (bf16[2,256,512]{2,1,0:T(8,128)(2,1)S(1)}, bf16[2,256,512]{2,1,0:T(8,128)(2,1)}, u32[]{:S(2)}) copy-start(bf16[2,256,512]{2,1,0:T(8,128)(2,1)} %param.12) | copy-start | bytes 1572868
  0.6 1.3 copy-start.1
  1.9 1.2 copy-start.2
  3.1 0.7 copy-start.3
  3.8 3.4 %copy-start.6 = (bf16[8,1792]{1,0:T(8,128)(2,1)S(1)}, bf16[8,1792]{1,0:T(8,128)(2,1)}, u32[]{:S(2)}) copy-start(bf16[8,1792]{1,0:T(8,128)(2,1)} %param.15) | copy-start | bytes 86020
  4.6 91.3 %collective-permute-start = (bf16[576,1792]{1,0:T(8,128)(2,1)S(1)}, bf16[576,1792]{1,0:T(8,128)(2,1)}, u32[]{:S(2)}, u32[]{:S(2)}) collective-permute-start(bf16[576,1792]{1,0:T(8,128)(2,1)S(1)} %get-tuple-element.12.own_ref), channel_id=1, source_target_pairs={{0,4},{4,0},{1,5},{5,1},{2,6},{6,2},{3,7},{7,3},{8,12},{12,8},{9,1... | collective-permute-start | bytes 6193160 | tf_op jit(solution)/shard_map/ppermute | solution.py:46
  95.9 4.8 %copy-start.7 = (bf16[2,64,256]{2,1,0:T(8,128)(2,1)S(1)}, bf16[2,64,256]{2,1,0:T(8,128)(2,1)}, u32[]{:S(2)}) copy-start(bf16[2,64,256]{2,1,0:T(8,128)(2,1)} %param.13) | copy-start | bytes 196612
  95.9 4.8 %copy-start.8 = (bf16[2,64,128]{2,1,0:T(8,128)(2,1)S(1)}, bf16[2,64,128]{2,1,0:T(8,128)(2,1)}, u32[]{:S(2)}) copy-start(bf16[2,64,128]{2,1,0:T(8,128)(2,1)} %param.11) | copy-start | bytes 98308
  95.9 5.1 %copy-start.9 = (s32[2]{0:T(128)S(1)}, s32[2]{0:T(128)}, u32[]{:S(2)}) copy-start(s32[2]{0:T(128)} %param.14) | copy-start | bytes 28
  95.9 5.1 %copy-start.5 = (bf16[2,128,512]{2,1,0:T(8,128)(2,1)S(1)}, bf16[2,128,512]{2,1,0:T(8,128)(2,1)}, u32[]{:S(2)}) copy-start(bf16[2,128,512]{2,1,0:T(8,128)(2,1)} %param.10) | copy-start | bytes 786436
  101.7 13.2 %all-to-all-start.1 = ((bf16[4,296,256]{2,1,0:T(8,128)(2,1)}), bf16[4,296,256]{2,1,0:T(8,128)(2,1)S(1)}, u32[]{:S(2)}, u32[]{:S(2)}) async-start(bf16[4,296,256]{2,1,0:T(8,128)(2,1)} %projected.1), calls=%async_computation.1 | async-start | bytes 1212416 | tf_op jit(solution)/shard_map/all_to_all | solution.py:50
  106.1 18.9 %collective-permute-start.1 = (bf16[288,1792]{1,0:T(8,128)(2,1)}, bf16[288,1792]{1,0:T(8,128)(2,1)S(1)}, u32[]{:S(2)}, u32[]{:S(2)}) collective-permute-start(bf16[288,1792]{1,0:T(8,128)(2,1)} %param.19), channel_id=1, source_target_pairs={{0,4},{4,0},{1,5},{5,1},{2,6},{6,2},{3,7},{7,3},{8,12},{12,8},{9,1... | collective-permute-start | bytes 3096584 | tf_op jit(solution)/shard_map/ppermute | solution.py:46
  115.8 9.2 %all-to-all-start.2 = ((bf16[4,2,72,256]{3,2,1,0:T(8,128)(2,1)}), bf16[4,2,72,256]{3,2,1,0:T(8,128)(2,1)S(1)}, u32[]{:S(2)}, u32[]{:S(2)}) async-start(bf16[4,2,72,256]{3,2,1,0:T(8,128)(2,1)} %broadcast_in_dim.31), calls=%async_computation.2 | async-start | bytes 589824 | tf_op jit(solution)/shard_map/all_to_all | solution.py:50
  120.4 5.3 %copy-start.4 = (bf16[288,1792]{1,0:T(8,128)(2,1)S(1)}, bf16[288,1792]{1,0:T(8,128)(2,1)}, u32[]{:S(2)}) copy-start(bf16[288,1792]{1,0:T(8,128)(2,1)} %param.19) | copy-start | bytes 3096580
  126.4 16.7 %collective-permute-start.4 = (bf16[8,8,1792]{2,1,0:T(8,128)(2,1)S(1)}, bf16[8,8,1792]{2,1,0:T(8,128)(2,1)S(1)}, u32[]{:S(2)}, u32[]{:S(2)}) collective-permute-start(bf16[8,8,1792]{2,1,0:T(8,128)(2,1)S(1)} %get-tuple-element.25), channel_id=1, source_target_pairs={{0,252},{12,0},{16,12},{28,16},{32,28},{44,32},{48,44},{60,48},{64... | collective-permute-start | bytes 688136 | tf_op jit(solution)/shard_map/ppermute | solution.py:36
  133.5 9.7 %collective-permute-start.3 = (bf16[8,8,1792]{2,1,0:T(8,128)(2,1)S(1)}, bf16[8,8,1792]{2,1,0:T(8,128)(2,1)S(1)}, u32[]{:S(2)}, u32[]{:S(2)}) collective-permute-start(bf16[8,8,1792]{2,1,0:T(8,128)(2,1)S(1)} %get-tuple-element.26), channel_id=1, source_target_pairs={{0,12},{12,16},{16,28},{28,32},{32,44},{44,48},{48,60},{60,64},{64... | collective-permute-start | bytes 688136 | tf_op jit(solution)/shard_map/ppermute | solution.py:36
  135.5 11.9 %collective-permute-start.2 = (bf16[8,8,1792]{2,1,0:T(8,128)(2,1)S(1)}, bf16[8,8,1792]{2,1,0:T(8,128)(2,1)S(1)}, u32[]{:S(2)}, u32[]{:S(2)}) collective-permute-start(bf16[8,8,1792]{2,1,0:T(8,128)(2,1)S(1)} %get-tuple-element.24), channel_id=1, source_target_pairs={{0,16},{12,28},{16,32},{28,44},{32,48},{44,60},{48,64},{60,76},{64... | collective-permute-start | bytes 688136 | tf_op jit(solution)/shard_map/ppermute | solution.py:36
  138.6 13.3 %all-to-all-start = ((bf16[4,2,32,640]{3,2,1,0:T(8,128)(2,1)}), bf16[4,2,32,640]{3,2,1,0:T(8,128)(2,1)S(1)}, u32[]{:S(2)}, u32[]{:S(2)}) async-start(bf16[4,2,32,640]{3,2,1,0:T(8,128)(2,1)} %bitcast.76), calls=%async_computation | async-start | bytes 655360 | tf_op jit(solution)/shard_map/all_to_all | solution.py:50
  147.6 11.0 %collective-permute-start.5 = (bf16[4,8,1792]{2,1,0:T(8,128)(2,1)S(1)}, bf16[4,8,1792]{2,1,0:T(8,128)(2,1)S(1)}, u32[]{:S(2)}, u32[]{:S(2)}) collective-permute-start(bf16[4,8,1792]{2,1,0:T(8,128)(2,1)S(1)} %dynamic-slice_bitcast_fusion.3), channel_id=1, source_target_pairs={{0,32},{12,44},{16,48},{28,60},{32,64},{44,76},{48,80},{60,92},{64... | collective-permute-start | bytes 344072 | tf_op jit(solution)/shard_map/ppermute | solution.py:36
  159.2 34.5 %all-to-all-start.3 = ((bf16[4,8,1792]{2,1,0:T(8,128)(2,1)}), bf16[4,8,1792]{2,1,0:T(8,128)(2,1)S(1)}, u32[]{:S(2)}, u32[]{:S(2)}) async-start(bf16[4,8,1792]{2,1,0:T(8,128)(2,1)} %fusion.9), calls=%async_computation.3 | async-start | bytes 229376 | tf_op jit(solution)/shard_map/all_to_all | solution.py:291
